TPU v7x, 256 devices: a whole 4x4x8 slice. The times are simulated.
256 devices in a mesh: seq: 64 (over y_hi, x, z), head: 4 (over y_lo, core).
Axes of the slice: x: 4, y: 4 (y_hi: 2, y_lo: 2; y = y_hi * 2 + y_lo), z: 8, core: 2. Of those that a mesh axis runs over, the one named last changes fastest.
Arguments:
- prompt_queries: bfloat16 [12288, 4096], P('seq', 'head'), may hold values from -16 to 16
- prompt_keys: bfloat16 [12288, 1024], P('seq', 'head'), may hold values from -16 to 16
- prompt_values: bfloat16 [12288, 1024], P('seq', 'head'), may hold values from -6 to 6
- span_offset: int32 [64], P('seq'), may hold values from 0 to 63, each once
- appended_queries: bfloat16 [64, 4096], P(None, 'head'), may hold values from -16 to 16
- appended_keys: bfloat16 [64, 1024], P(None, 'head'), may hold values from -6 to 6
- appended_values: bfloat16 [64, 1024], P(None, 'head'), may hold values from -6 to 6
- dec_pos: int32 [64], replicated, may hold values from 2 to 12288, as said below
- out_weight: bfloat16 [4096, 4096], P('head'), may hold values from -0.09375 to 0.09375
Outputs:
- layer_out: bfloat16 [12288, 4096], P(('seq', 'head'))
- dec_out: bfloat16 [64, 4096], P('seq', 'head')
Inputs may be any that keep to these rules, and one draw needn't show every extreme that they name: span_offset is a permutation of 0 to 63. `dec_pos`: some appended token stands at 12288 in every draw.
All inputs are finite; a program needn't handle non-finite values.
Results may differ from a plain program's by a relative error of at most 0.015.
Values may be sent and summed in bfloat16 or wider, within the bound.
No kernel may reach another device: no remote copies, remote signals or barrier semaphores. Data moves between devices by JAX's collectives and lax.ppermute only.
A program may use at most 256 MiB of HBM per device.

v0:
```python
from functools import partial
import math

import jax
import jax.numpy as jnp
from jax import lax
from jax.experimental import pallas as pl
from jax.experimental.pallas import tpu as pltpu
from jax.sharding import Mesh, PartitionSpec as P


HEAD_SIZE = 128
T = 192
TP = T + 8
G = 4
R = G * T
ACC = HEAD_SIZE + 8
NB = 16
LOW = -1e30
EMPTY = -1e29
SCALE = HEAD_SIZE**-0.5 * math.log2(math.e)


def shift(x, axis, k):
    n = lax.axis_size(axis)
    return lax.ppermute(x, axis, [((i + k) % n, i) for i in range(n)])


def rounded(x):
    return x.astype(jnp.bfloat16).astype(jnp.float32)


def spec(space=pltpu.VMEM):
    return pl.BlockSpec(memory_space=space)


def params():
    return pltpu.CompilerParams(vmem_limit_bytes=24 << 20)


def position_tile(offset, width):
    return jnp.full((8, width), offset[0], jnp.int32).astype(jnp.float32).astype(jnp.bfloat16)


def pack_kv_body(offset, k, v, mine, other):
    yh = lax.axis_index("yh")
    tile = position_tile(offset, 256)
    for out, head in ((mine, yh), (other, 1 - yh)):
        at = pl.multiple_of(head * HEAD_SIZE, HEAD_SIZE)
        out[0:T, 0:HEAD_SIZE] = k[:, pl.ds(at, HEAD_SIZE)]
        out[0:T, HEAD_SIZE:] = v[:, pl.ds(at, HEAD_SIZE)]
        out[T:TP, :] = tile


def pack_q_body(offset, q, mine, other):
    yh = lax.axis_index("yh")
    tile = position_tile(offset, 512)
    for out, head in ((mine, yh), (other, 1 - yh)):
        out[0:T, :] = q[:, pl.ds(pl.multiple_of(head * 512, 512), 512)]
        out[T:TP, :] = tile


def pack(body, width, offset, *arrays):
    return pl.pallas_call(
        body,
        in_specs=[spec(pltpu.SMEM)] + [spec()] * len(arrays),
        out_specs=[spec()] * 2,
        out_shape=[jax.ShapeDtypeStruct((TP, width), jnp.bfloat16)] * 2,
        compiler_params=params(),
        name="pack",
    )(offset, *arrays)


def dec_step(q, blocks, acc, top, total):
    scores = []
    high = top
    for k, _, seen in blocks:
        s = lax.dot_general(
            q, k, (((1,), (1,)), ((), ())), preferred_element_type=jnp.float32
        )
        s = jnp.where(seen, s * SCALE, LOW)
        scores.append(s)
        high = jnp.maximum(high, rounded(jnp.max(s, axis=1, keepdims=True)))
    factor = jnp.exp2(top - high)
    total, acc = total * factor, acc * factor
    for s, (_, v, seen) in zip(scores, blocks):
        w = jnp.where(seen, jnp.exp2(s - high), 0.0)
        total = total + jnp.sum(w, axis=1, keepdims=True)
        acc = acc + jnp.dot(w.astype(jnp.bfloat16), v, preferred_element_type=jnp.float32)
    return acc, high, total


def sort_blocks(pieces, kv, table, limit):
    keys = lax.broadcasted_iota(jnp.int32, (32, T), 1)
    where = []
    for ref in pieces:
        for at in (0, TP):
            tag = ref[at + T : at + TP, 0:128].astype(jnp.float32)
            where.append((ref, at, jnp.max(tag).astype(jnp.int32)))
    blocks = []
    for ref, at, pos in where:
        rank = sum((other < pos).astype(jnp.int32) for _, _, other in where)
        block = ref[at : at + T, :]
        kv[pl.ds(pl.multiple_of(rank * T, T), T), :] = block
        table[rank] = pos
        blocks.append((block[:, :HEAD_SIZE], block[:, HEAD_SIZE:], keys + pos * T < limit))
    return blocks


def early_body(dq, sk, sv, dpos, *refs):
    pieces, state = refs[:-1], refs[-1]
    q = dq[...]
    limit = dpos[:, 0:1]
    keys = lax.broadcasted_iota(jnp.int32, (32, T), 1)
    blocks = []
    for ref in pieces:
        for at in (0, TP):
            pos = ref[at + T : at + T + 1, 0:1].astype(jnp.float32).astype(jnp.int32)
            block = ref[at : at + T, :]
            blocks.append((block[:, :HEAD_SIZE], block[:, HEAD_SIZE:], keys + pos * T < limit))
    own = lax.broadcasted_iota(jnp.int32, (32, 1), 0) < 8
    score = jnp.sum(q.astype(jnp.float32) * sk[...].astype(jnp.float32), axis=1, keepdims=True)
    score = jnp.where(own, score * SCALE, LOW)
    top = rounded(score)
    weight = jnp.where(own, jnp.exp2(score - top), 0.0)
    acc = rounded(weight) * sv[...].astype(jnp.float32)
    acc, top, total = dec_step(q, blocks, acc, top, weight)
    state[0:32, :] = acc
    state[32:64, :] = jnp.broadcast_to(top, (32, HEAD_SIZE))
    state[64:96, :] = jnp.broadcast_to(total, (32, HEAD_SIZE))


def early(small, pieces):
    return pl.pallas_call(
        early_body,
        in_specs=[spec()] * (len(small) + len(pieces)),
        out_specs=spec(),
        out_shape=jax.ShapeDtypeStruct((96, HEAD_SIZE), jnp.float32),
        compiler_params=params(),
        name="early",
    )(*small, *pieces)


def gather_body(early_blocks, dq, state, dpos, *refs):
    pieces, (kv, table, dec) = refs[:-3], refs[-3:]
    blocks = sort_blocks(pieces, kv, table, dpos[:, 0:1])[early_blocks:]
    acc, top, total = dec_step(
        dq[...], blocks, state[0:32, :], state[32:64, 0:1], state[64:96, 0:1]
    )
    rows = lax.broadcasted_iota(jnp.int32, (8, R), 0)
    top = jnp.broadcast_to(top, (32, HEAD_SIZE))
    total = jnp.broadcast_to(total, (32, HEAD_SIZE))
    for n in range(8):

        def row(a):
            parts = [a[n * G + h : n * G + h + 1, :] for h in range(G)]
            flat = jnp.concatenate(parts + [jnp.zeros((1, 256), jnp.float32)], axis=1)
            return jnp.broadcast_to(flat, (8, R))

        tile = jnp.where(rows == 2, row(acc), 0.0)
        tile = jnp.where(rows == 3, row(top), tile)
        tile = jnp.where(rows == 4, row(total), tile)
        dec[n] = tile


def gather(early_blocks, small, pieces):
    return pl.pallas_call(
        partial(gather_body, early_blocks),
        in_specs=[spec()] * (len(small) + len(pieces)),
        out_specs=[spec(), spec(pltpu.SMEM), spec()],
        out_shape=[
            jax.ShapeDtypeStruct((NB * T, 256), jnp.bfloat16),
            jax.ShapeDtypeStruct((NB,), jnp.int32),
            jax.ShapeDtypeStruct((8, 8, R), jnp.float32),
        ],
        compiler_params=params(),
        name="gather",
    )(*small, *pieces)


W = 256
SPREAD = 60.0


def attend_body(groups, table, *refs):
    n = len(groups)
    queries, (kv, dec), outs = refs[:n], refs[n : n + 2], refs[n + 2 : 2 * n + 2]
    qs, acc, stat, positions, again = refs[2 * n + 2 :]
    for i, q in enumerate(queries):
        for b in range(2):
            at = b * TP
            for h in range(G):
                qs[2 * i + b, h * T : (h + 1) * T, :] = q[
                    at : at + T, h * HEAD_SIZE : (h + 1) * HEAD_SIZE
                ]
            tag = q[at + T : at + TP, 0:128].astype(jnp.float32)
            positions[2 * i + b] = jnp.max(tag).astype(jnp.int32)
    rows = lax.broadcasted_iota(jnp.int32, (8, R), 0)
    cols = list(range(0, R, W))

    @pl.loop(0, n)
    def _(turn):
        counts, sames = [], []
        for b in range(2):
            pos = positions[2 * turn + b]
            count = jnp.int32(0)
            same = jnp.int32(0)
            for m in range(NB):
                count = count + (table[m] < pos).astype(jnp.int32)
                same = same + (table[m] == pos).astype(jnp.int32)
            counts.append(count)
            sames.append(same)
        rests = [c + s for c, s in zip(counts, sames)]

        def read(first, blocks, b):
            at = pl.multiple_of(first * T, T)
            k = kv[pl.ds(at, blocks * T), 0:HEAD_SIZE]
            v = kv[pl.ds(at, blocks * T), HEAD_SIZE:]
            scores = [
                lax.dot_general(
                    k,
                    qs[2 * turn + b, c : c + W, :],
                    (((1,), (1,)), ((), ())),
                    preferred_element_type=jnp.float32,
                )
                for c in cols
            ]
            return v, scores

        def apply(v, w):
            return lax.dot_general(
                v,
                w.astype(jnp.bfloat16),
                (((0,), (0,)), ((), ())),
                preferred_element_type=jnp.float32,
            )

        def exact(fours, i):
            reads = []
            for b in range(2):
                first = jnp.minimum(4 * fours[b] + 2 * i, NB - 2)
                live = 4 * fours[b] + 2 * i < rests[b]
                seen = jnp.where(live, (counts[b] - first) * T, -2 * NB * T)
                reads.append((seen, *read(first, 2, b)))
            for n, c in enumerate(cols):
                row = lax.broadcasted_iota(jnp.int32, (1, W), 1) + c
                for edge in (3 * T, 2 * T, T):
                    row = jnp.where(row >= edge, row - edge, row)
                key = lax.broadcasted_iota(jnp.int32, (2 * T, W), 0)
                for b, (seen, v, scores) in enumerate(reads):
                    limit = jnp.where(sames[b] > 0, row, -1) + seen
                    s = jnp.where(key <= limit, scores[n] * SCALE, LOW)
                    old = stat[b, 0:1, c : c + W]
                    high = jnp.maximum(old, rounded(jnp.max(s, axis=0, keepdims=True)))
                    factor = jnp.exp2(old - high)
                    w = jnp.exp2(s - high)
                    stat[b, 0:1, c : c + W] = high
                    stat[b, 1:2, c : c + W] = stat[b, 1:2, c : c + W] * factor + jnp.sum(
                        w, axis=0, keepdims=True
                    )
                    acc[b, :, c : c + W] = acc[b, :, c : c + W] * factor + apply(v, w)

        def quick(first, which):
            reads = [(b, *read(first, 4, b)) for b in which]
            for n, c in enumerate(cols):
                for b, v, scores in reads:
                    s = scores[n] * SCALE
                    w = jnp.exp2(s - stat[b, 0:1, c : c + W])
                    stat[b, 2:3, c : c + W] = jnp.maximum(
                        stat[b, 2:3, c : c + W], jnp.max(s, axis=0, keepdims=True)
                    )
                    stat[b, 1:2, c : c + W] = stat[b, 1:2, c : c + W] + jnp.sum(
                        w, axis=0, keepdims=True
                    )
                    acc[b, :, c : c + W] = acc[b, :, c : c + W] + apply(v, w)

        again[0] = jnp.int32(1)

        @pl.loop(0, 2)
        def _(attempt):
            @pl.when(again[0] == 1)
            def _():
                fours = [
                    jnp.where(attempt == 0, jnp.maximum(rest - 1, 0) // 4, 0) for rest in rests
                ]
                acc[...] = jnp.zeros_like(acc)
                for b in range(2):
                    stat[b] = jnp.where(rows == 1, 0.0, EMPTY)
                left = [(rest - 4 * f + 1) // 2 for rest, f in zip(rests, fours)]

                @pl.loop(0, jnp.maximum(left[0], left[1]))
                def _(i):
                    exact(fours, i)

                both = jnp.minimum(fours[0], fours[1])
                longer = (fours[1] > fours[0]).astype(jnp.int32)

                @pl.loop(0, both)
                def _(i):
                    quick(4 * i, (0, 1))

                @pl.loop(both, jnp.maximum(fours[0], fours[1]))
                def _(i):
                    quick(4 * i, (longer,))

                over = jnp.maximum(
                    jnp.max(stat[0, 2:3, :] - stat[0, 0:1, :]),
                    jnp.max(stat[1, 2:3, :] - stat[1, 0:1, :]),
                )
                again[0] = (over > SPREAD).astype(jnp.int32)

        for i, (out, group) in enumerate(zip(outs, groups)):

            @pl.when(turn == i)
            def _():
                for b in range(2):
                    out[b, 0:HEAD_SIZE, :] = acc[b].astype(jnp.bfloat16)
                    tile = jnp.where(rows < 2, stat[b], dec[2 * group + b])
                    out[b, HEAD_SIZE:, :] = tile.astype(jnp.bfloat16)


def attend_call(table, queries, kv, dec, groups):
    n = len(groups)
    return pl.pallas_call(
        partial(attend_body, groups),
        in_specs=[spec(pltpu.SMEM)] + [spec()] * (n + 2),
        out_specs=[spec()] * n,
        out_shape=[jax.ShapeDtypeStruct((2, ACC, R), jnp.bfloat16)] * n,
        scratch_shapes=[
            pltpu.VMEM((2 * n, R, HEAD_SIZE), jnp.bfloat16),
            pltpu.VMEM((2, HEAD_SIZE, R), jnp.float32),
            pltpu.VMEM((2, 8, R), jnp.float32),
            pltpu.SMEM((2 * n,), jnp.int32),
            pltpu.SMEM((1,), jnp.int32),
        ],
        cost_estimate=pl.CostEstimate(
            flops=2 * n * NB * T * R * HEAD_SIZE * 4,
            bytes_accessed=4 << 20,
            transcendentals=2 * n * NB * T * R,
        ),
        compiler_params=params(),
        name="attend",
    )(table, *queries, kv, dec)


def merge_body(*refs):
    core = lax.axis_index("c")
    parts, outs, turned = refs[:4], refs[4:8], refs[8]
    for b in range(2):
        stats = [p[b, HEAD_SIZE:, :].astype(jnp.float32) for p in parts]
        high = stats[0][0:1, :]
        for s in stats[1:]:
            high = jnp.maximum(high, s[0:1, :])
        factors = [jnp.exp2(s[0:1, :] - high) for s in stats]
        total = sum(f * s[1:2, :] for f, s in zip(factors, stats))
        acc = sum(
            f * p[b, 0:HEAD_SIZE, :].astype(jnp.float32) for f, p in zip(factors, parts)
        )
        flat = acc / total
        for h in range(G):
            head = flat[:, h * T : (h + 1) * T].T
            turned[:, h * HEAD_SIZE : (h + 1) * HEAD_SIZE] = head.astype(jnp.bfloat16)
        high = stats[0][3:4, :512]
        for s in stats[1:]:
            high = jnp.maximum(high, s[3:4, :512])
        factors = [jnp.exp2(s[3:4, :512] - high) for s in stats]
        total = sum(f * s[4:5, :512] for f, s in zip(factors, stats))
        acc = sum(f * s[2:3, :512] for f, s in zip(factors, stats))
        row = jnp.broadcast_to(acc / total, (8, 512)).astype(jnp.bfloat16)
        for other in range(2):
            out = outs[2 * b + other]
            start = core * 48 if other == 0 else (1 - core) * 48
            for half in range(2):
                rows = pl.ds(pl.multiple_of(start + 96 * half, 16), 48)
                out[half * 48 : half * 48 + 48, :] = turned[rows, :]
            out[96:104, :] = row


def merge(parts):
    return pl.pallas_call(
        merge_body,
        in_specs=[spec()] * 4,
        out_specs=[spec()] * 4,
        out_shape=[jax.ShapeDtypeStruct((104, 512), jnp.bfloat16)] * 4,
        scratch_shapes=[pltpu.VMEM((T, 512), jnp.bfloat16)],
        compiler_params=params(),
        name="merge",
    )(*parts)


def layer(q, k, v, span_offset, appended_q, appended_k, appended_v, dec_pos, out_weight):
    yh, x, z = (lax.axis_index(a) for a in ("yh", "x", "z"))
    yl, c = lax.axis_index("yl"), lax.axis_index("c")
    kv_mine, kv_other = pack(pack_kv_body, 256, span_offset, k, v)
    q_mine, q_other = pack(pack_q_body, 512, span_offset, q)
    kv_pair = jnp.concatenate([kv_mine, shift(kv_other, "yh", 1)], axis=0)
    q_pair = jnp.concatenate([q_mine, shift(q_other, "yh", 1)], axis=0)

    other_weight = shift(out_weight, "c", 1)

    tokens = jnp.stack(
        [
            jnp.bitwise_xor(yh, b) * 32 + ((x + g) % 4) * 8 + z
            for g in range(4)
            for b in range(2)
        ]
    ).astype(jnp.int32)
    pick = (tokens[:, None] == jnp.arange(64, dtype=jnp.int32)[None, :]).astype(jnp.bfloat16)

    def rows_of(a):
        w = a.shape[1] // 2
        a = jnp.where(yh == 0, a[:, :w], a[:, w:])
        return jnp.dot(pick, a, preferred_element_type=jnp.float32).astype(jnp.bfloat16)

    dq = rows_of(appended_q).reshape(32, HEAD_SIZE)
    sk = jnp.repeat(rows_of(appended_k), G, axis=0)
    sv = jnp.repeat(rows_of(appended_v), G, axis=0)
    dpos = jnp.sum(jnp.where(tokens[:, None] == jnp.arange(64)[None, :], dec_pos[None, :], 0), axis=1)
    dpos = jnp.broadcast_to(jnp.repeat(dpos, G)[:, None], (32, 128)).astype(jnp.int32)

    f1, b1 = shift(kv_pair, "z", 1), shift(kv_pair, "z", -1)
    f1, b1, dq, sk, sv, dpos = lax.optimization_barrier((f1, b1, dq, sk, sv, dpos))
    f2, b2 = shift(f1, "z", 1), shift(b1, "z", -1)
    groups = [q_pair, shift(q_pair, "x", 1), shift(q_pair, "x", 2), shift(q_pair, "x", -1)]
    state = early([dq, sk, sv, dpos], [kv_pair, f1, b1])
    f3, b3 = shift(f2, "z", 1), shift(b2, "z", -1)
    f4 = shift(f3, "z", 1)
    kv, table, dec = gather(6, [dq, state, dpos], [kv_pair, f1, b1, f2, b2, f3, b3, f4])
    table, other_weight = lax.optimization_barrier((table, other_weight))
    (far,) = attend_call(table, [groups[2]], kv, dec, [2])
    table, far = lax.optimization_barrier((table, far))
    back2 = shift(far, "x", 2)
    ahead, behind = attend_call(table, [groups[1], groups[3]], kv, dec, [1, 3])
    table, ahead, behind = lax.optimization_barrier((table, ahead, behind))
    back1 = shift(ahead, "x", -1)
    back3 = shift(behind, "x", 1)
    (own,) = attend_call(table, [groups[0]], kv, dec, [0])

    mine, by_core, by_pair, by_both = merge([own, back1, back2, back3])
    by_core = shift(by_core, "c", 1)
    by_pair = shift(by_pair, "yh", 1)
    by_both = lax.ppermute(by_both, ("yh", "c"), [(i, 3 - i) for i in range(4)])
    first = yh == 0

    def ordered(a, b):
        return jnp.concatenate([jnp.where(first, a, b), jnp.where(first, b, a)], axis=1)

    here, there = ordered(mine, by_pair), ordered(by_core, by_both)
    result = jnp.dot(here, out_weight, preferred_element_type=jnp.float32)
    result = result + jnp.dot(there, other_weight, preferred_element_type=jnp.float32)
    low, high, tail = result[:48], result[48:96], result[96:]
    low_here = yl == 0
    send = jnp.where(low_here, high, low)
    keep = jnp.where(low_here, low, high)
    arrived = shift(jnp.concatenate([send, tail], axis=0).astype(jnp.bfloat16), "yl", 1)
    layer_out = (keep + arrived[:48].astype(jnp.float32)).astype(jnp.bfloat16)
    tail = tail[0] + arrived[48].astype(jnp.float32)
    dec_out = lax.dynamic_slice_in_dim(tail, (yl * 2 + c) * 1024, 1024)[None]
    return layer_out, dec_out.astype(jnp.bfloat16)


def solution(mesh):
    fine = Mesh(mesh.devices.reshape(2, 4, 8, 2, 2), ("yh", "x", "z", "yl", "c"))
    seq, head = ("yh", "x", "z"), ("yl", "c")
    in_specs = (
        P(seq, head),
        P(seq, head),
        P(seq, head),
        P(seq),
        P(None, head),
        P(None, head),
        P(None, head),
        P(),
        P(head, None),
    )
    out_specs = (P(seq + head, None), P(seq, head))
    return jax.shard_map(layer, mesh=fine, in_specs=in_specs, out_specs=out_specs, check_vma=False)
```

profile of v0, /device:TPU:1, one launch (start us, length us, event | category | flops | bytes accessed | tf_op | source)
XLA Modules:
  0.0 115.2 jit_solution(18427652352103438063)
XLA Ops:
  0.6 3.3 %collective-permute-start.8 = (bf16[1024,4096]{1,0:T(8,128)(2,1)}, bf16[1024,4096]{1,0:T(8,128)(2,1)}, u32[]{:S(2)}, u32[]{:S(2)}) collective-permute-start(bf16[1024,4096]{1,0:T(8,128)(2,1)} %param.17), channel_id=1, source_target_pairs={{1,0},{0,1},{3,2},{2,3},{5,4},{4,5},{7,6},{6,7},{9,8},{8,9},{11,10... | collective-permute-start | bytes 25165832 | tf_op jit(solution)/shard_map/ppermute | solution.py:26
  4.6 0.9 copy-done.1
  5.5 0.9 copy-done.2
  6.4 1.3 %collective-permute-start = (bf16[200,256]{1,0:T(8,128)(2,1)S(1)}, bf16[200,256]{1,0:T(8,128)(2,1)S(1)}, u32[]{:S(2)}, u32[]{:S(2)}) collective-permute-start(bf16[200,256]{1,0:T(8,128)(2,1)S(1)} %get-tuple-element.29), channel_id=1, source_target_pairs={{128,0},{0,128},{129,1},{1,129},{130,2},{2,130},{131,3},{3,131},{1... | collective-permute-start | bytes 307208 | tf_op jit(solution)/shard_map/ppermute | solution.py:26
  7.7 0.1 stack.35
  7.8 1.1 convolution_convert_fusion
  8.9 0.8 select_reduce_fusion
  9.7 0.1 broadcast_in_dim.38
  9.8 0.1 broadcast_in_dim.39
  9.9 1.0 copy-done
  10.9 0.9 convolution_convert_fusion.2
  11.8 0.6 collective-permute-done
  12.4 5.1 %collective-permute-start.1 = (bf16[400,256]{1,0:T(8,128)(2,1)S(1)}, bf16[400,256]{1,0:T(8,128)(2,1)S(1)}, u32[]{:S(2)}, u32[]{:S(2)}) collective-permute-start(bf16[400,256]{1,0:T(8,128)(2,1)S(1)} %constant_dynamic-update-slice_fusion.refs_0_), channel_id=1, source_target_pairs={{4,0},{8,4},{12,8},{16,12},{20,16},{24,20},{28,24},{0,28},{5,1},{9... | collective-permute-start | bytes 614408 | tf_op jit(solution)/shard_map/ppermute | solution.py:26
  17.5 0.0 collective-permute-start.2
  17.5 0.9 convolution_convert_fusion.1
  18.4 3.2 %collective-permute-done.1.refs_1_ = bf16[400,256]{1,0:T(8,128)(2,1)S(1)} collective-permute-done((bf16[400,256]{1,0:T(8,128)(2,1)S(1)}, bf16[400,256]{1,0:T(8,128)(2,1)S(1)}, u32[]{:S(2)}, u32[]{:S(2)}) %collective-permute-start.1) | collective-permute-done | bytes 204832 | tf_op jit(solution)/shard_map/ppermute | solution.py:26
  21.7 3.1 %collective-permute-done.2.refs_2_ = bf16[400,256]{1,0:T(8,128)(2,1)S(1)} collective-permute-done((bf16[400,256]{1,0:T(8,128)(2,1)S(1)}, bf16[400,256]{1,0:T(8,128)(2,1)S(1)}, u32[]{:S(2)}, u32[]{:S(2)}) %collective-permute-start.2) | collective-permute-done | bytes 204832 | tf_op jit(solution)/shard_map/ppermute | solution.py:26
  24.8 0.1 broadcast_in_dim.40.dpos
  24.9 0.3 collective-permute-start.3
  25.2 1.2 %collective-permute-start.9 = (bf16[200,512]{1,0:T(8,128)(2,1)S(1)}, bf16[200,512]{1,0:T(8,128)(2,1)S(1)}, u32[]{:S(2)}, u32[]{:S(2)}) collective-permute-start(bf16[200,512]{1,0:T(8,128)(2,1)S(1)} %get-tuple-element.39), channel_id=1, source_target_pairs={{128,0},{0,128},{129,1},{1,129},{130,2},{2,130},{131,3},{3,131},{1... | collective-permute-start | bytes 614408 | tf_op jit(solution)/shard_map/ppermute | solution.py:26
  26.4 1.2 %collective-permute-start.4 = (bf16[400,256]{1,0:T(8,128)(2,1)S(1)}, bf16[400,256]{1,0:T(8,128)(2,1)S(1)}, u32[]{:S(2)}, u32[]{:S(2)}) collective-permute-start(bf16[400,256]{1,0:T(8,128)(2,1)S(1)} %collective-permute-done.2.refs_2_), channel_id=1, source_target_pairs={{28,0},{0,4},{4,8},{8,12},{12,16},{16,20},{20,24},{24,28},{29,1},{... | collective-permute-start | bytes 614408 | tf_op jit(solution)/shard_map/ppermute | solution.py:26
  27.6 2.5 %collective-permute-done.3.refs_3_ = bf16[400,256]{1,0:T(8,128)(2,1)S(1)} collective-permute-done((bf16[400,256]{1,0:T(8,128)(2,1)S(1)}, bf16[400,256]{1,0:T(8,128)(2,1)S(1)}, u32[]{:S(2)}, u32[]{:S(2)}) %collective-permute-start.3) | collective-permute-done | bytes 204832 | tf_op jit(solution)/shard_map/ppermute | solution.py:26
  30.1 1.8 %collective-permute-start.5 = (bf16[400,256]{1,0:T(8,128)(2,1)S(1)}, bf16[400,256]{1,0:T(8,128)(2,1)S(1)}, u32[]{:S(2)}, u32[]{:S(2)}) collective-permute-start(bf16[400,256]{1,0:T(8,128)(2,1)S(1)} %collective-permute-done.3.refs_3_), channel_id=1, source_target_pairs={{4,0},{8,4},{12,8},{16,12},{20,16},{24,20},{28,24},{0,28},{5,1},{9... | collective-permute-start | bytes 614408 | tf_op jit(solution)/shard_map/ppermute | solution.py:26
  31.9 0.0 collective-permute-done.9
  31.9 2.8 %collective-permute-start.10 = (bf16[400,512]{1,0:T(8,128)(2,1)S(1)}, bf16[400,512]{1,0:T(8,128)(2,1)S(1)}, u32[]{:S(2)}, u32[]{:S(2)}) collective-permute-start(bf16[400,512]{1,0:T(8,128)(2,1)S(1)} %constant_dynamic-update-slice_fusion.2.refs_0_), channel_id=1, source_target_pairs={{64,0},{96,32},{0,64},{32,96},{65,1},{97,33},{1,65},{33,97},{66,2}... | collective-permute-start | bytes 1228808 | tf_op jit(solution)/shard_map/ppermute | solution.py:26
  34.7 0.0 collective-permute-done.4.refs_4_
  34.7 0.9 collective-permute-start.6
  35.6 0.0 collective-permute-done.5.refs_5_
  35.6 2.1 %collective-permute-start.7 = (bf16[400,256]{1,0:T(8,128)(2,1)S(1)}, bf16[400,256]{1,0:T(8,128)(2,1)S(1)}, u32[]{:S(2)}, u32[]{:S(2)}) collective-permute-start(bf16[400,256]{1,0:T(8,128)(2,1)S(1)} %collective-permute-done.5.refs_5_), channel_id=1, source_target_pairs={{4,0},{8,4},{12,8},{16,12},{20,16},{24,20},{28,24},{0,28},{5,1},{9... | collective-permute-start | bytes 614408 | tf_op jit(solution)/shard_map/ppermute | solution.py:26
  37.7 2.5 %collective-permute-start.11 = (bf16[400,512]{1,0:T(8,128)(2,1)S(1)}, bf16[400,512]{1,0:T(8,128)(2,1)S(1)}, u32[]{:S(2)}, u32[]{:S(2)}) collective-permute-start(bf16[400,512]{1,0:T(8,128)(2,1)S(1)} %constant_dynamic-update-slice_fusion.2.refs_0_), channel_id=1, source_target_pairs={{32,0},{64,32},{96,64},{0,96},{33,1},{65,33},{97,65},{1,97},{34,2}... | collective-permute-start | bytes 1228808 | tf_op jit(solution)/shard_map/ppermute | solution.py:26
  40.2 0.7 collective-permute-done.6.refs_6_
  40.9 0.2 collective-permute-start.12
  41.0 0.7 early.1.state
  41.7 0.0 collective-permute-done.7.refs_7_
  41.7 1.4 %gather.1 = (bf16[3072,256]{1,0:T(8,128)(2,1)S(1)}, s32[16]{0:T(128)S(1)}, f32[8,8,768]{2,1,0:T(8,128)S(1)}) custom-call(bf16[32,128]{1,0:T(8,128)(2,1)S(1)} %reshape.22.dq, f32[96,128]{1,0:T(8,128)S(1)} %early.1.state, s32[32,128]{1,0:T(8,128)S(1)} %broadcast_in_dim.40.dpos, bf16[400,256]{1,0:T(8,128)(2,1)S(1)} %constant_dynamic-update-slice_fusion.refs_0_, ...), custom_call_target="tpu_custom_call" | custom-call | tf_op jit(solution)/shard_map/gather/pallas_call | solution.py:167
  43.1 0.0 collective-permute-done.8
  43.1 0.0 collective-permute-done.10.refs_0_
  43.1 5.7 %attend.3 = bf16[2,136,768]{2,1,0:T(8,128)(2,1)S(1)} custom-call(s32[16]{0:T(128)S(1)} %get-tuple-element.45.table, bf16[400,512]{1,0:T(8,128)(2,1)S(1)} %collective-permute-done.10.refs_0_, bf16[3072,256]{1,0:T(8,128)(2,1)S(1)} %get-tuple-element.40.refs_1_.refs_2_, f32[8,8,768]{2,1,0:T(8,128)S(1)} %get-tuple-element.41.refs_2_.refs_3_), custom_call_target="tpu_custom_call" | custom-call | flops 2415919104 | bytes 4194304 | tf_op jit(solution)/shard_map/attend/pallas_call | solution.py:324
  48.8 2.4 %collective-permute-done.11.refs_0_ = bf16[400,512]{1,0:T(8,128)(2,1)S(1)} collective-permute-done((bf16[400,512]{1,0:T(8,128)(2,1)S(1)}, bf16[400,512]{1,0:T(8,128)(2,1)S(1)}, u32[]{:S(2)}, u32[]{:S(2)}) %collective-permute-start.11) | collective-permute-done | bytes 409632 | tf_op jit(solution)/shard_map/ppermute | solution.py:26
  51.2 0.0 collective-permute-done.12.refs_1_
  51.2 7.6 %attend.4 = (bf16[2,136,768]{2,1,0:T(8,128)(2,1)S(1)}, bf16[2,136,768]{2,1,0:T(8,128)(2,1)S(1)}) custom-call(s32[16]{0:T(128)S(1)} %get-tuple-element.45.table, bf16[400,512]{1,0:T(8,128)(2,1)S(1)} %collective-permute-done.11.refs_0_, bf16[400,512]{1,0:T(8,128)(2,1)S(1)} %collective-permute-done.12.refs_1_, ...), custom_call_target="tpu_custom_call" | custom-call | flops 4831838208 | bytes 4194304 | tf_op jit(solution)/shard_map/attend/pallas_call | solution.py:324
  58.8 7.6 %collective-permute-start.13 = (bf16[2,136,768]{2,1,0:T(8,128)(2,1)S(1)}, bf16[2,136,768]{2,1,0:T(8,128)(2,1)S(1)}, u32[]{:S(2)}, u32[]{:S(2)}) collective-permute-start(bf16[2,136,768]{2,1,0:T(8,128)(2,1)S(1)} %get-tuple-element.46), channel_id=1, source_target_pairs={{96,0},{0,32},{32,64},{64,96},{97,1},{1,33},{33,65},{65,97},{98,2}... | collective-permute-start | bytes 1253384 | tf_op jit(solution)/shard_map/ppermute | solution.py:26
  66.4 0.0 collective-permute-start.14
  66.4 2.5 %collective-permute-start.15 = (bf16[2,136,768]{2,1,0:T(8,128)(2,1)S(1)}, bf16[2,136,768]{2,1,0:T(8,128)(2,1)S(1)}, u32[]{:S(2)}, u32[]{:S(2)}) collective-permute-start(bf16[2,136,768]{2,1,0:T(8,128)(2,1)S(1)} %get-tuple-element.48), channel_id=1, source_target_pairs={{32,0},{64,32},{96,64},{0,96},{33,1},{65,33},{97,65},{1,97},{34,2}... | collective-permute-start | bytes 1253384 | tf_op jit(solution)/shard_map/ppermute | solution.py:26
  68.9 6.0 %attend.5.refs_0_ = bf16[2,136,768]{2,1,0:T(8,128)(2,1)S(1)} custom-call(s32[16]{0:T(128)S(1)} %get-tuple-element.45.table, bf16[400,512]{1,0:T(8,128)(2,1)S(1)} %constant_dynamic-update-slice_fusion.2.refs_0_, bf16[3072,256]{1,0:T(8,128)(2,1)S(1)} %get-tuple-element.40.refs_1_.refs_2_, f32[8,8,768]{2,1,0:T(8,128)S(1)} %get-tuple-element.41.refs_2_.refs_3_), custom_call_target="tpu_custom_call" | custom-call | flops 2415919104 | bytes 4194304 | tf_op jit(solution)/shard_map/attend/pallas_call | solution.py:324
  74.9 0.0 collective-permute-done.13.refs_1_
  74.9 8.0 %collective-permute-done.14.refs_2_ = bf16[2,136,768]{2,1,0:T(8,128)(2,1)S(1)} collective-permute-done((bf16[2,136,768]{2,1,0:T(8,128)(2,1)S(1)}, bf16[2,136,768]{2,1,0:T(8,128)(2,1)S(1)}, u32[]{:S(2)}, u32[]{:S(2)}) %collective-permute-start.14) | collective-permute-done | bytes 417824 | tf_op jit(solution)/shard_map/ppermute | solution.py:26
  82.9 1.6 %collective-permute-done.15.refs_3_ = bf16[2,136,768]{2,1,0:T(8,128)(2,1)S(1)} collective-permute-done((bf16[2,136,768]{2,1,0:T(8,128)(2,1)S(1)}, bf16[2,136,768]{2,1,0:T(8,128)(2,1)S(1)}, u32[]{:S(2)}, u32[]{:S(2)}) %collective-permute-start.15) | collective-permute-done | bytes 417824 | tf_op jit(solution)/shard_map/ppermute | solution.py:26
  84.6 0.7 merge.1
  85.3 1.6 %collective-permute-start.17 = (bf16[104,512]{1,0:T(8,128)(2,1)S(1)}, bf16[104,512]{1,0:T(8,128)(2,1)S(1)}, u32[]{:S(2)}, u32[]{:S(2)}) collective-permute-start(bf16[104,512]{1,0:T(8,128)(2,1)S(1)} %get-tuple-element.51), channel_id=1, source_target_pairs={{1,0},{0,1},{3,2},{2,3},{5,4},{4,5},{7,6},{6,7},{9,8},{8,9},{11,10... | collective-permute-start | bytes 319496 | tf_op jit(solution)/shard_map/ppermute | solution.py:26
  86.9 0.0 collective-permute-start.18
  86.9 3.0 %collective-permute-start.16 = (bf16[104,512]{1,0:T(8,128)(2,1)S(1)}, bf16[104,512]{1,0:T(8,128)(2,1)S(1)}, u32[]{:S(2)}, u32[]{:S(2)}) collective-permute-start(bf16[104,512]{1,0:T(8,128)(2,1)S(1)} %get-tuple-element.50), channel_id=1, source_target_pairs={{128,0},{0,128},{129,1},{1,129},{130,2},{2,130},{131,3},{3,131},{1... | collective-permute-start | bytes 319496 | tf_op jit(solution)/shard_map/ppermute | solution.py:26
  89.8 0.0 collective-permute-done.17
  89.9 3.8 %collective-permute-done.18 = bf16[104,512]{1,0:T(8,128)(2,1)S(1)} collective-permute-done((bf16[104,512]{1,0:T(8,128)(2,1)S(1)}, bf16[104,512]{1,0:T(8,128)(2,1)S(1)}, u32[]{:S(2)}, u32[]{:S(2)}) %collective-permute-start.18) | collective-permute-done | bytes 106528 | tf_op jit(solution)/shard_map/ppermute | solution.py:442
  93.7 0.0 slice-start.1
  93.7 4.9 %fusion.3 = f32[104,4096]{1,0:T(8,128)S(1)} fusion(bf16[1024,4096]{1,0:T(8,128)(2,1)} %collective-permute-done.8, bf16[104,512]{1,0:T(8,128)(2,1)S(1)} %get-tuple-element.57, bf16[104,512]{1,0:T(8,128)(2,1)S(1)} %get-tuple-element.56), kind=kOutput, calls=%fused_computation.10 | convolution fusion | flops 872841216 | bytes 10305536 | tf_op jit(solution)/shard_map/dot_general | solution.py:450
  98.6 0.0 collective-permute-done.16
  98.7 0.9 slice-done.1
  99.5 1.5 %convolution_add_fusion = f32[104,4096]{1,0:T(8,128)S(1)} fusion(f32[104,4096]{1,0:T(8,128)S(1)} %fusion.3, bf16[1024,4096]{1,0:T(8,128)(2,1)S(1)} %bitcast.15, bf16[104,512]{1,0:T(8,128)(2,1)S(1)} %get-tuple-element.55, bf16[104,512]{1,0:T(8,128)(2,1)S(1)} %get-tuple-element.54), kind=kOutput, calls=%fused_computation | convolution fusion | flops 873267200 | bytes 12009472 | tf_op jit(solution)/shard_map/dot_general | solution.py:449
  101.0 0.1 select_convert_fusion
  101.1 0.1 collective-permute-start.19
  101.3 12.4 %collective-permute-done.19 = bf16[56,4096]{1,0:T(8,128)(2,1)S(1)} collective-permute-done((bf16[56,4096]{1,0:T(8,128)(2,1)S(1)}, bf16[56,4096]{1,0:T(8,128)(2,1)S(1)}, u32[]{:S(2)}, u32[]{:S(2)}) %collective-permute-start.19) | collective-permute-done | bytes 458784 | tf_op jit(solution)/shard_map/ppermute | solution.py:26
  113.7 0.6 fusion.19
  114.3 0.8 add_convert_fusion
  (21 shorter events, 0.3 us)
Async XLA Ops:
  0.6 42.4 %collective-permute-start.8 = (bf16[1024,4096]{1,0:T(8,128)(2,1)}, bf16[1024,4096]{1,0:T(8,128)(2,1)}, u32[]{:S(2)}, u32[]{:S(2)}) collective-permute-start(bf16[1024,4096]{1,0:T(8,128)(2,1)} %param.17), channel_id=1, source_target_pairs={{1,0},{0,1},{3,2},{2,3},{5,4},{4,5},{7,6},{6,7},{9,8},{8,9},{11,10... | collective-permute-start | bytes 25165832 | tf_op jit(solution)/shard_map/ppermute | solution.py:26
  4.6 0.9 copy-start.1
  5.5 0.9 copy-start.2
  6.4 6.0 %collective-permute-start = (bf16[200,256]{1,0:T(8,128)(2,1)S(1)}, bf16[200,256]{1,0:T(8,128)(2,1)S(1)}, u32[]{:S(2)}, u32[]{:S(2)}) collective-permute-start(bf16[200,256]{1,0:T(8,128)(2,1)S(1)} %get-tuple-element.29), channel_id=1, source_target_pairs={{128,0},{0,128},{129,1},{1,129},{130,2},{2,130},{131,3},{3,131},{1... | collective-permute-start | bytes 307208 | tf_op jit(solution)/shard_map/ppermute | solution.py:26
  9.9 1.0 copy-start
  12.4 9.2 %collective-permute-start.1 = (bf16[400,256]{1,0:T(8,128)(2,1)S(1)}, bf16[400,256]{1,0:T(8,128)(2,1)S(1)}, u32[]{:S(2)}, u32[]{:S(2)}) collective-permute-start(bf16[400,256]{1,0:T(8,128)(2,1)S(1)} %constant_dynamic-update-slice_fusion.refs_0_), channel_id=1, source_target_pairs={{4,0},{8,4},{12,8},{16,12},{20,16},{24,20},{28,24},{0,28},{5,1},{9... | collective-permute-start | bytes 614408 | tf_op jit(solution)/shard_map/ppermute | solution.py:26
  17.5 7.3 %collective-permute-start.2 = (bf16[400,256]{1,0:T(8,128)(2,1)S(1)}, bf16[400,256]{1,0:T(8,128)(2,1)S(1)}, u32[]{:S(2)}, u32[]{:S(2)}) collective-permute-start(bf16[400,256]{1,0:T(8,128)(2,1)S(1)} %constant_dynamic-update-slice_fusion.refs_0_), channel_id=1, source_target_pairs={{28,0},{0,4},{4,8},{8,12},{12,16},{16,20},{20,24},{24,28},{29,1},{... | collective-permute-start | bytes 614408 | tf_op jit(solution)/shard_map/ppermute | solution.py:26
  24.9 5.2 %collective-permute-start.3 = (bf16[400,256]{1,0:T(8,128)(2,1)S(1)}, bf16[400,256]{1,0:T(8,128)(2,1)S(1)}, u32[]{:S(2)}, u32[]{:S(2)}) collective-permute-start(bf16[400,256]{1,0:T(8,128)(2,1)S(1)} %collective-permute-done.1.refs_1_), channel_id=1, source_target_pairs={{4,0},{8,4},{12,8},{16,12},{20,16},{24,20},{28,24},{0,28},{5,1},{9... | collective-permute-start | bytes 614408 | tf_op jit(solution)/shard_map/ppermute | solution.py:26
  25.2 6.7 %collective-permute-start.9 = (bf16[200,512]{1,0:T(8,128)(2,1)S(1)}, bf16[200,512]{1,0:T(8,128)(2,1)S(1)}, u32[]{:S(2)}, u32[]{:S(2)}) collective-permute-start(bf16[200,512]{1,0:T(8,128)(2,1)S(1)} %get-tuple-element.39), channel_id=1, source_target_pairs={{128,0},{0,128},{129,1},{1,129},{130,2},{2,130},{131,3},{3,131},{1... | collective-permute-start | bytes 614408 | tf_op jit(solution)/shard_map/ppermute | solution.py:26
  26.4 8.4 %collective-permute-start.4 = (bf16[400,256]{1,0:T(8,128)(2,1)S(1)}, bf16[400,256]{1,0:T(8,128)(2,1)S(1)}, u32[]{:S(2)}, u32[]{:S(2)}) collective-permute-start(bf16[400,256]{1,0:T(8,128)(2,1)S(1)} %collective-permute-done.2.refs_2_), channel_id=1, source_target_pairs={{28,0},{0,4},{4,8},{8,12},{12,16},{16,20},{20,24},{24,28},{29,1},{... | collective-permute-start | bytes 614408 | tf_op jit(solution)/shard_map/ppermute | solution.py:26
  30.1 5.5 %collective-permute-start.5 = (bf16[400,256]{1,0:T(8,128)(2,1)S(1)}, bf16[400,256]{1,0:T(8,128)(2,1)S(1)}, u32[]{:S(2)}, u32[]{:S(2)}) collective-permute-start(bf16[400,256]{1,0:T(8,128)(2,1)S(1)} %collective-permute-done.3.refs_3_), channel_id=1, source_target_pairs={{4,0},{8,4},{12,8},{16,12},{20,16},{24,20},{28,24},{0,28},{5,1},{9... | collective-permute-start | bytes 614408 | tf_op jit(solution)/shard_map/ppermute | solution.py:26
  31.9 11.2 %collective-permute-start.10 = (bf16[400,512]{1,0:T(8,128)(2,1)S(1)}, bf16[400,512]{1,0:T(8,128)(2,1)S(1)}, u32[]{:S(2)}, u32[]{:S(2)}) collective-permute-start(bf16[400,512]{1,0:T(8,128)(2,1)S(1)} %constant_dynamic-update-slice_fusion.2.refs_0_), channel_id=1, source_target_pairs={{64,0},{96,32},{0,64},{32,96},{65,1},{97,33},{1,65},{33,97},{66,2}... | collective-permute-start | bytes 1228808 | tf_op jit(solution)/shard_map/ppermute | solution.py:26
  34.7 6.1 %collective-permute-start.6 = (bf16[400,256]{1,0:T(8,128)(2,1)S(1)}, bf16[400,256]{1,0:T(8,128)(2,1)S(1)}, u32[]{:S(2)}, u32[]{:S(2)}) collective-permute-start(bf16[400,256]{1,0:T(8,128)(2,1)S(1)} %collective-permute-done.4.refs_4_), channel_id=1, source_target_pairs={{28,0},{0,4},{4,8},{8,12},{12,16},{16,20},{20,24},{24,28},{29,1},{... | collective-permute-start | bytes 614408 | tf_op jit(solution)/shard_map/ppermute | solution.py:26
  35.6 6.0 %collective-permute-start.7 = (bf16[400,256]{1,0:T(8,128)(2,1)S(1)}, bf16[400,256]{1,0:T(8,128)(2,1)S(1)}, u32[]{:S(2)}, u32[]{:S(2)}) collective-permute-start(bf16[400,256]{1,0:T(8,128)(2,1)S(1)} %collective-permute-done.5.refs_5_), channel_id=1, source_target_pairs={{4,0},{8,4},{12,8},{16,12},{20,16},{24,20},{28,24},{0,28},{5,1},{9... | collective-permute-start | bytes 614408 | tf_op jit(solution)/shard_map/ppermute | solution.py:26
  37.7 13.5 %collective-permute-start.11 = (bf16[400,512]{1,0:T(8,128)(2,1)S(1)}, bf16[400,512]{1,0:T(8,128)(2,1)S(1)}, u32[]{:S(2)}, u32[]{:S(2)}) collective-permute-start(bf16[400,512]{1,0:T(8,128)(2,1)S(1)} %constant_dynamic-update-slice_fusion.2.refs_0_), channel_id=1, source_target_pairs={{32,0},{64,32},{96,64},{0,96},{33,1},{65,33},{97,65},{1,97},{34,2}... | collective-permute-start | bytes 1228808 | tf_op jit(solution)/shard_map/ppermute | solution.py:26
  40.9 10.3 %collective-permute-start.12 = (bf16[400,512]{1,0:T(8,128)(2,1)S(1)}, bf16[400,512]{1,0:T(8,128)(2,1)S(1)}, u32[]{:S(2)}, u32[]{:S(2)}) collective-permute-start(bf16[400,512]{1,0:T(8,128)(2,1)S(1)} %constant_dynamic-update-slice_fusion.2.refs_0_), channel_id=1, source_target_pairs={{96,0},{0,32},{32,64},{64,96},{97,1},{1,33},{33,65},{65,97},{98,2}... | collective-permute-start | bytes 1228808 | tf_op jit(solution)/shard_map/ppermute | solution.py:26
  58.8 16.1 %collective-permute-start.13 = (bf16[2,136,768]{2,1,0:T(8,128)(2,1)S(1)}, bf16[2,136,768]{2,1,0:T(8,128)(2,1)S(1)}, u32[]{:S(2)}, u32[]{:S(2)}) collective-permute-start(bf16[2,136,768]{2,1,0:T(8,128)(2,1)S(1)} %get-tuple-element.46), channel_id=1, source_target_pairs={{96,0},{0,32},{32,64},{64,96},{97,1},{1,33},{33,65},{65,97},{98,2}... | collective-permute-start | bytes 1253384 | tf_op jit(solution)/shard_map/ppermute | solution.py:26
  66.4 16.5 %collective-permute-start.14 = (bf16[2,136,768]{2,1,0:T(8,128)(2,1)S(1)}, bf16[2,136,768]{2,1,0:T(8,128)(2,1)S(1)}, u32[]{:S(2)}, u32[]{:S(2)}) collective-permute-start(bf16[2,136,768]{2,1,0:T(8,128)(2,1)S(1)} %attend.3), channel_id=1, source_target_pairs={{64,0},{96,32},{0,64},{32,96},{65,1},{97,33},{1,65},{33,97},{66,2}... | collective-permute-start | bytes 1253384 | tf_op jit(solution)/shard_map/ppermute | solution.py:26
  66.4 18.1 %collective-permute-start.15 = (bf16[2,136,768]{2,1,0:T(8,128)(2,1)S(1)}, bf16[2,136,768]{2,1,0:T(8,128)(2,1)S(1)}, u32[]{:S(2)}, u32[]{:S(2)}) collective-permute-start(bf16[2,136,768]{2,1,0:T(8,128)(2,1)S(1)} %get-tuple-element.48), channel_id=1, source_target_pairs={{32,0},{64,32},{96,64},{0,96},{33,1},{65,33},{97,65},{1,97},{34,2}... | collective-permute-start | bytes 1253384 | tf_op jit(solution)/shard_map/ppermute | solution.py:26
  85.3 4.6 %collective-permute-start.17 = (bf16[104,512]{1,0:T(8,128)(2,1)S(1)}, bf16[104,512]{1,0:T(8,128)(2,1)S(1)}, u32[]{:S(2)}, u32[]{:S(2)}) collective-permute-start(bf16[104,512]{1,0:T(8,128)(2,1)S(1)} %get-tuple-element.51), channel_id=1, source_target_pairs={{1,0},{0,1},{3,2},{2,3},{5,4},{4,5},{7,6},{6,7},{9,8},{8,9},{11,10... | collective-permute-start | bytes 319496 | tf_op jit(solution)/shard_map/ppermute | solution.py:26
  86.9 6.8 %collective-permute-start.18 = (bf16[104,512]{1,0:T(8,128)(2,1)S(1)}, bf16[104,512]{1,0:T(8,128)(2,1)S(1)}, u32[]{:S(2)}, u32[]{:S(2)}) collective-permute-start(bf16[104,512]{1,0:T(8,128)(2,1)S(1)} %get-tuple-element.52), channel_id=1, source_target_pairs={{0,129},{1,128},{128,1},{129,0},{2,131},{3,130},{130,3},{131,2},{4... | collective-permute-start | bytes 319496 | tf_op jit(solution)/shard_map/ppermute | solution.py:442
  86.9 11.7 %collective-permute-start.16 = (bf16[104,512]{1,0:T(8,128)(2,1)S(1)}, bf16[104,512]{1,0:T(8,128)(2,1)S(1)}, u32[]{:S(2)}, u32[]{:S(2)}) collective-permute-start(bf16[104,512]{1,0:T(8,128)(2,1)S(1)} %get-tuple-element.50), channel_id=1, source_target_pairs={{128,0},{0,128},{129,1},{1,129},{130,2},{2,130},{131,3},{3,131},{1... | collective-permute-start | bytes 319496 | tf_op jit(solution)/shard_map/ppermute | solution.py:26
  93.7 5.0 %slice-start = ((s8[8388608]{0:T(1024)(128)(4,1)}), s8[4194304]{0:T(1024)(128)(4,1)S(1)}, s32[]{:S(2)}) async-start(s8[8388608]{0:T(1024)(128)(4,1)} %bitcast.14), calls=%async_computation | async-start | bytes 8388608
  93.7 5.8 %slice-start.1 = ((s8[8388608]{0:T(1024)(128)(4,1)}), s8[4194304]{0:T(1024)(128)(4,1)S(1)}, s32[]{:S(2)}) async-start(s8[8388608]{0:T(1024)(128)(4,1)} %bitcast.14), calls=%async_computation.1 | async-start | bytes 8388608
  101.1 12.6 %collective-permute-start.19 = (bf16[56,4096]{1,0:T(8,128)(2,1)S(1)}, bf16[56,4096]{1,0:T(8,128)(2,1)S(1)}, u32[]{:S(2)}, u32[]{:S(2)}) collective-permute-start(bf16[56,4096]{1,0:T(8,128)(2,1)S(1)} %pad_maximum_fusion), channel_id=1, source_target_pairs={{2,0},{0,2},{3,1},{1,3},{6,4},{4,6},{7,5},{5,7},{10,8},{8,10},{11,... | collective-permute-start | bytes 1376264 | tf_op jit(solution)/shard_map/ppermute | solution.py:26
where the time goes:
time: 116 us; the launch traced here: 115 us
  waiting for transfers between devices  38.5 us (33%)
  starting transfers between devices  37.4 us (32%)
  Pallas kernels  22.1 us (19%)
  matrix products  9.27 us (8%)
  local copies, waits for them, and re-layouts  4.08 us (4%)
  other arithmetic  2.44 us (2%)
  between operations  1.5 us (1%)
    ppermute x19, starting transfers between devices, shift(): return lax.ppermute(x, axis, [((i + k) % n, i) for i in range(n)])  37.4 us
    ppermute x19, waiting for transfers between devices, shift(): return lax.ppermute(x, axis, [((i + k) % n, i) for i in range(n)])  34.7 us
    pallas_call x3, Pallas kernels, attend_call(): pl.pallas_call(partial(attend_body, groups), in_specs=[spec(pltpu.SMEM)]...  19.3 us
    dot_general x1, matrix products, layer(): jnp.dot(there, other_weight, preferred_element_type=jnp.float32)  4.89 us
    ppermute x1, waiting for transfers between devices, layer(): by_both = lax.ppermute(by_both, ('yh', 'c'), [(i, 3 - i) for i in range(4)])  3.81 us
    unnamed x12, local copies, waits for them, and re-layouts  3.68 us
    dot_general x3, matrix products, rows_of(): jnp.dot(pick, a, preferred_element_type=jnp.float32).astype(jnp.bfloat16)  2.9 us
  transfers between devices with their start and end apart: 20, of which 10 were waited for; matrix products, arithmetic and copies ran while one was open for 8% of the time, Pallas kernels for 12%

commit v1 on v0

--- a/solution.py
+++ b/solution.py
@@ -38,37 +38,43 @@
     return pltpu.CompilerParams(vmem_limit_bytes=24 << 20)
 
 
-def position_tile(offset, width):
-    return jnp.full((8, width), offset[0], jnp.int32).astype(jnp.float32).astype(jnp.bfloat16)
-
-
-def pack_kv_body(offset, k, v, mine, other):
+def pack_body(offset, q, k, v, kv_mine, kv_other, q_mine, q_other, sems):
     yh = lax.axis_index("yh")
-    tile = position_tile(offset, 256)
-    for out, head in ((mine, yh), (other, 1 - yh)):
-        at = pl.multiple_of(head * HEAD_SIZE, HEAD_SIZE)
-        out[0:T, 0:HEAD_SIZE] = k[:, pl.ds(at, HEAD_SIZE)]
-        out[0:T, HEAD_SIZE:] = v[:, pl.ds(at, HEAD_SIZE)]
-        out[T:TP, :] = tile
-
-
-def pack_q_body(offset, q, mine, other):
-    yh = lax.axis_index("yh")
-    tile = position_tile(offset, 512)
-    for out, head in ((mine, yh), (other, 1 - yh)):
-        out[0:T, :] = q[:, pl.ds(pl.multiple_of(head * 512, 512), 512)]
-        out[T:TP, :] = tile
-
-
-def pack(body, width, offset, *arrays):
-    return pl.pallas_call(
-        body,
-        in_specs=[spec(pltpu.SMEM)] + [spec()] * len(arrays),
-        out_specs=[spec()] * 2,
-        out_shape=[jax.ShapeDtypeStruct((TP, width), jnp.bfloat16)] * 2,
+    copies = []
+
+    def copy(source, width, head, target, at):
+        cols = pl.ds(pl.multiple_of(head * width, width), width)
+        copies.append(
+            pltpu.make_async_copy(
+                source.at[:, cols], target.at[0:T, at : at + width], sems.at[len(copies)]
+            )
+        )
+        copies[-1].start()
+
+    for kv, qq, head in ((kv_other, q_other, 1 - yh), (kv_mine, q_mine, yh)):
+        copy(k, HEAD_SIZE, head, kv, 0)
+        copy(v, HEAD_SIZE, head, kv, HEAD_SIZE)
+        copy(q, 512, head, qq, 0)
+    tile = jnp.full((8, 512), offset[0], jnp.int32).astype(jnp.float32).astype(jnp.bfloat16)
+    for kv, qq in ((kv_mine, q_mine), (kv_other, q_other)):
+        kv[T:TP, :] = tile[:, :256]
+        qq[T:TP, :] = tile
+    for c in copies:
+        c.wait()
+
+
+def pack(offset, q, k, v):
+    return pl.pallas_call(
+        pack_body,
+        in_specs=[spec(pltpu.SMEM)] + [spec(pltpu.HBM)] * 3,
+        out_specs=[spec()] * 4,
+        out_shape=[
+            jax.ShapeDtypeStruct((TP, width), jnp.bfloat16) for width in (256, 256, 512, 512)
+        ],
+        scratch_shapes=[pltpu.SemaphoreType.DMA((6,))],
         compiler_params=params(),
         name="pack",
-    )(offset, *arrays)
+    )(offset, q, k, v)
 
 
 def dec_step(q, blocks, acc, top, total):
@@ -388,16 +394,111 @@
     )(*parts)
 
 
+def fetch_body(source, target, sems):
+    copies = []
+    for n in range(8):
+        rows = pl.ds(n * 128, 128)
+        copies.append(pltpu.make_async_copy(source.at[rows], target.at[rows], sems.at[n]))
+        copies[-1].start()
+    for c in copies:
+        c.wait()
+
+
+def fetch(w):
+    return pl.pallas_call(
+        fetch_body,
+        in_specs=[spec(pltpu.HBM)],
+        out_specs=spec(),
+        out_shape=jax.ShapeDtypeStruct(w.shape, w.dtype),
+        scratch_shapes=[pltpu.SemaphoreType.DMA((8,))],
+        compiler_params=params(),
+        name="fetch",
+    )(w)
+
+
+def project_body(half, mine, by_pair, by_core, by_both, w, other_w, *refs):
+    send, keep = refs[-2:]
+    yh, low_here = lax.axis_index("yh"), lax.axis_index("yl") == 0
+    here = pl.ds(pl.multiple_of(yh * 512, 512), 512)
+    there = pl.ds(pl.multiple_of((1 - yh) * 512, 512), 512)
+    for n in range(0, 2048, 512):
+        cols = slice(half * 2048 + n, half * 2048 + n + 512)
+        result = sum(
+            jnp.dot(a[...], b[rows, cols], preferred_element_type=jnp.float32)
+            for a, b, rows in (
+                (mine, w, here),
+                (by_core, other_w, here),
+                (by_pair, w, there),
+                (by_both, other_w, there),
+            )
+        )
+        low, high, tail = result[:48], result[48:96], result[96:]
+        send[:48, n : n + 512] = jnp.where(low_here, high, low).astype(jnp.bfloat16)
+        keep[:48, n : n + 512] = jnp.where(low_here, low, high)
+        keep[48:, n : n + 512] = tail
+    if half == 1:
+        tail = jnp.where(low_here, keep[48:49, :], refs[0][48:49, :])
+        tail = jnp.where(lax.axis_index("c") == 0, tail[:, :1024], tail[:, 1024:])
+        parts = [tail[:, n * 128 : n * 128 + 128] for n in range(8)]
+        send[0:8, 2048:] = jnp.concatenate(parts, axis=0).astype(jnp.bfloat16)
+        send[8:48, 2048:] = jnp.zeros((40, 128), jnp.bfloat16)
+
+
+def project(half, *operands):
+    return pl.pallas_call(
+        partial(project_body, half),
+        in_specs=[spec()] * len(operands),
+        out_specs=[spec()] * 2,
+        out_shape=[
+            jax.ShapeDtypeStruct((48, 2048 + 128 * half), jnp.bfloat16),
+            jax.ShapeDtypeStruct((56, 2048), jnp.float32),
+        ],
+        cost_estimate=pl.CostEstimate(
+            flops=104 * 2048 * 2048 * 2, bytes_accessed=9 << 20, transcendentals=0
+        ),
+        compiler_params=params(),
+        name="project",
+    )(*operands)
+
+
+def close_body(keep_0, keep_1, arrived_0, arrived_1, layer_out, dec_out):
+    for half, (keep, arrived) in enumerate(((keep_0, arrived_0), (keep_1, arrived_1))):
+        result = keep[:48, :] + arrived[:, :2048].astype(jnp.float32)
+        layer_out[:, half * 2048 : half * 2048 + 2048] = result.astype(jnp.bfloat16)
+    tail = jnp.where(lax.axis_index("yl") == 0, keep_0[48:49, :], keep_1[48:49, :])
+    tail = jnp.where(lax.axis_index("c") == 0, tail[:, :1024], tail[:, 1024:])
+    other = arrived_1[0:8, 2048:].astype(jnp.float32)
+    other = jnp.concatenate([other[n : n + 1, :] for n in range(8)], axis=1)
+    dec_out[...] = (tail + other).astype(jnp.bfloat16)
+
+
+def close(*operands):
+    return pl.pallas_call(
+        close_body,
+        in_specs=[spec()] * 4,
+        out_specs=[spec()] * 2,
+        out_shape=[
+            jax.ShapeDtypeStruct((48, 4096), jnp.bfloat16),
+            jax.ShapeDtypeStruct((1, 1024), jnp.bfloat16),
+        ],
+        compiler_params=params(),
+        name="close",
+    )(*operands)
+
+
 def layer(q, k, v, span_offset, appended_q, appended_k, appended_v, dec_pos, out_weight):
     yh, x, z = (lax.axis_index(a) for a in ("yh", "x", "z"))
-    yl, c = lax.axis_index("yl"), lax.axis_index("c")
-    kv_mine, kv_other = pack(pack_kv_body, 256, span_offset, k, v)
-    q_mine, q_other = pack(pack_q_body, 512, span_offset, q)
+    kv_mine, kv_other, q_mine, q_other = pack(span_offset, q, k, v)
     kv_pair = jnp.concatenate([kv_mine, shift(kv_other, "yh", 1)], axis=0)
     q_pair = jnp.concatenate([q_mine, shift(q_other, "yh", 1)], axis=0)
 
-    other_weight = shift(out_weight, "c", 1)
-
+    other_weight = fetch(shift(out_weight, "c", 1))
+
+    f1, b1 = shift(kv_pair, "z", 1), shift(kv_pair, "z", -1)
+    f2, b2 = shift(f1, "z", 1), shift(b1, "z", -1)
+    f2, b2, appended_q, appended_k, appended_v, dec_pos = lax.optimization_barrier(
+        (f2, b2, appended_q, appended_k, appended_v, dec_pos)
+    )
     tokens = jnp.stack(
         [
             jnp.bitwise_xor(yh, b) * 32 + ((x + g) % 4) * 8 + z
@@ -418,9 +519,6 @@
     dpos = jnp.sum(jnp.where(tokens[:, None] == jnp.arange(64)[None, :], dec_pos[None, :], 0), axis=1)
     dpos = jnp.broadcast_to(jnp.repeat(dpos, G)[:, None], (32, 128)).astype(jnp.int32)
 
-    f1, b1 = shift(kv_pair, "z", 1), shift(kv_pair, "z", -1)
-    f1, b1, dq, sk, sv, dpos = lax.optimization_barrier((f1, b1, dq, sk, sv, dpos))
-    f2, b2 = shift(f1, "z", 1), shift(b1, "z", -1)
     groups = [q_pair, shift(q_pair, "x", 1), shift(q_pair, "x", 2), shift(q_pair, "x", -1)]
     state = early([dq, sk, sv, dpos], [kv_pair, f1, b1])
     f3, b3 = shift(f2, "z", 1), shift(b2, "z", -1)
@@ -440,23 +538,13 @@
     by_core = shift(by_core, "c", 1)
     by_pair = shift(by_pair, "yh", 1)
     by_both = lax.ppermute(by_both, ("yh", "c"), [(i, 3 - i) for i in range(4)])
-    first = yh == 0
-
-    def ordered(a, b):
-        return jnp.concatenate([jnp.where(first, a, b), jnp.where(first, b, a)], axis=1)
-
-    here, there = ordered(mine, by_pair), ordered(by_core, by_both)
-    result = jnp.dot(here, out_weight, preferred_element_type=jnp.float32)
-    result = result + jnp.dot(there, other_weight, preferred_element_type=jnp.float32)
-    low, high, tail = result[:48], result[48:96], result[96:]
-    low_here = yl == 0
-    send = jnp.where(low_here, high, low)
-    keep = jnp.where(low_here, low, high)
-    arrived = shift(jnp.concatenate([send, tail], axis=0).astype(jnp.bfloat16), "yl", 1)
-    layer_out = (keep + arrived[:48].astype(jnp.float32)).astype(jnp.bfloat16)
-    tail = tail[0] + arrived[48].astype(jnp.float32)
-    dec_out = lax.dynamic_slice_in_dim(tail, (yl * 2 + c) * 1024, 1024)[None]
-    return layer_out, dec_out.astype(jnp.bfloat16)
+    pieces = (mine, by_pair, by_core, by_both)
+    send_0, keep_0 = project(0, *pieces, out_weight, other_weight)
+    send_0, keep_0, *pieces = lax.optimization_barrier((send_0, keep_0, *pieces))
+    arrived_0 = shift(send_0, "yl", 1)
+    send_1, keep_1 = project(1, *pieces, out_weight, other_weight, keep_0)
+    arrived_1 = shift(send_1, "yl", 1)
+    return close(keep_0, keep_1, arrived_0, arrived_1)
 
 
 def solution(mesh):

time: 116 us -> 112 us (0.966)
  Pallas kernels: 22.1 us -> 29.4 us
  matrix products: 9.27 us -> 2.9 us
  waiting for transfers between devices: 38.5 us -> 34.3 us
  other arithmetic: 2.44 us -> 0.84 us
  starting transfers between devices: 37.4 us -> 38.6 us
    pallas_call x2 -> x5, Pallas kernels: 0.07 us -> 7.39 us  [the longest x1 3.48 us: fetch(): pl.pallas_call(fetch_body, in_specs=[spec(pltpu.HBM)], out_specs=spec(),...]
    dot_general x2 -> x0, matrix products: 6.37 us -> none  [the longest x1 4.89 us: layer(): jnp.dot(there, other_weight, preferred_element_type=jnp.float32)]
    ppermute x19 -> x20, waiting for transfers between devices: 34.7 us -> 29.2 us  [shift(): return lax.ppermute(x, axis, [((i + k) % n, i) for i in range(n)])]
    convert_element_type x2 -> x0, other arithmetic: 1.45 us -> none  [the longest x1 0.84 us: layer(): layer_out = (keep + arrived[:48].astype(jnp.float32)).astype(jnp.bfloat16)]
    ppermute x1, waiting for transfers between devices: 3.81 us -> 5.13 us  [layer(): by_both = lax.ppermute(by_both, ('yh', 'c'), [(i, 3 - i) for i in range(4)])]
    ppermute x19 -> x20, starting transfers between devices: 37.4 us -> 38.6 us  [shift(): return lax.ppermute(x, axis, [((i + k) % n, i) for i in range(n)])]
  transfers between devices with their start and end apart: 20 -> 21, of which waited for: 10 -> 10; matrix products, arithmetic and copies ran while one was open for 8% -> 4% of each run, Pallas kernels for 12% -> 16%
where the time goes in v1:
time: 112 us; the launch traced here: 111 us
  starting transfers between devices  38.6 us (34%)
  waiting for transfers between devices  34.3 us (31%)
  Pallas kernels  29.4 us (26%)
  local copies, waits for them, and re-layouts  3.17 us (3%)
  matrix products  2.9 us (3%)
  between operations  1.48 us (1%)
    ppermute x20, starting transfers between devices, shift(): return lax.ppermute(x, axis, [((i + k) % n, i) for i in range(n)])  38.6 us
    ppermute x20, waiting for transfers between devices, shift(): return lax.ppermute(x, axis, [((i + k) % n, i) for i in range(n)])  29.2 us
    pallas_call x3, Pallas kernels, attend_call(): pl.pallas_call(partial(attend_body, groups), in_specs=[spec(pltpu.SMEM)]...  19.3 us
    ppermute x1, waiting for transfers between devices, layer(): by_both = lax.ppermute(by_both, ('yh', 'c'), [(i, 3 - i) for i in range(4)])  5.13 us
    pallas_call x1, Pallas kernels, fetch(): pl.pallas_call(fetch_body, in_specs=[spec(pltpu.HBM)], out_specs=spec(),...  3.48 us
    pallas_call x2, Pallas kernels, project(): pl.pallas_call(partial(project_body, half), in_specs=[spec()] * len(opera...  2.92 us
    dot_general x3, matrix products, rows_of(): jnp.dot(pick, a, preferred_element_type=jnp.float32).astype(jnp.bfloat16)  2.9 us
    unnamed x12, local copies, waits for them, and re-layouts  2.81 us
  transfers between devices with their start and end apart: 21, of which 10 were waited for; matrix products, arithmetic and copies ran while one was open for 4% of the time, Pallas kernels for 16%

profile of v1, /device:TPU:1, one launch (start us, length us, event | category | flops | bytes accessed | tf_op | source)
XLA Modules:
  0.0 110.6 jit_solution(640288053890009)
XLA Ops:
  0.6 3.3 %collective-permute-start.8 = (bf16[1024,4096]{1,0:T(8,128)(2,1)}, bf16[1024,4096]{1,0:T(8,128)(2,1)}, u32[]{:S(2)}, u32[]{:S(2)}) collective-permute-start(bf16[1024,4096]{1,0:T(8,128)(2,1)} %w.3), channel_id=1, source_target_pairs={{1,0},{0,1},{3,2},{2,3},{5,4},{4,5},{7,6},{6,7},{9,8},{8,9},{11,10... | collective-permute-start | bytes 25165832 | tf_op jit(solution)/shard_map/ppermute | solution.py:26
  4.6 1.0 copy-done
  5.6 0.9 copy-done.1
  6.5 0.9 copy-done.2
  7.4 0.2 pack.1
  7.5 1.3 %collective-permute-start = (bf16[200,256]{1,0:T(8,128)(2,1)S(1)}, bf16[200,256]{1,0:T(8,128)(2,1)S(1)}, u32[]{:S(2)}, u32[]{:S(2)}) collective-permute-start(bf16[200,256]{1,0:T(8,128)(2,1)S(1)} %get-tuple-element.39), channel_id=1, source_target_pairs={{128,0},{0,128},{129,1},{1,129},{130,2},{2,130},{131,3},{3,131},{1... | collective-permute-start | bytes 307208 | tf_op jit(solution)/shard_map/ppermute | solution.py:26
  8.8 4.7 %collective-permute-done = bf16[200,256]{1,0:T(8,128)(2,1)S(1)} collective-permute-done((bf16[200,256]{1,0:T(8,128)(2,1)S(1)}, bf16[200,256]{1,0:T(8,128)(2,1)S(1)}, u32[]{:S(2)}, u32[]{:S(2)}) %collective-permute-start) | collective-permute-done | bytes 102432 | tf_op jit(solution)/shard_map/ppermute | solution.py:26
  13.6 3.9 %collective-permute-start.1 = (bf16[400,256]{1,0:T(8,128)(2,1)S(1)}, bf16[400,256]{1,0:T(8,128)(2,1)S(1)}, u32[]{:S(2)}, u32[]{:S(2)}) collective-permute-start(bf16[400,256]{1,0:T(8,128)(2,1)S(1)} %constant_dynamic-update-slice_fusion.refs_0_), channel_id=1, source_target_pairs={{4,0},{8,4},{12,8},{16,12},{20,16},{24,20},{28,24},{0,28},{5,1},{9... | collective-permute-start | bytes 614408 | tf_op jit(solution)/shard_map/ppermute | solution.py:26
  17.5 0.0 collective-permute-start.3
  17.5 2.9 %collective-permute-start.9 = (bf16[200,512]{1,0:T(8,128)(2,1)S(1)}, bf16[200,512]{1,0:T(8,128)(2,1)S(1)}, u32[]{:S(2)}, u32[]{:S(2)}) collective-permute-start(bf16[200,512]{1,0:T(8,128)(2,1)S(1)} %get-tuple-element.49), channel_id=1, source_target_pairs={{128,0},{0,128},{129,1},{1,129},{130,2},{2,130},{131,3},{3,131},{1... | collective-permute-start | bytes 614408 | tf_op jit(solution)/shard_map/ppermute | solution.py:26
  20.4 0.1 stack.35
  20.5 0.6 collective-permute-done.1.refs_1_
  21.1 3.4 %collective-permute-start.2 = (bf16[400,256]{1,0:T(8,128)(2,1)S(1)}, bf16[400,256]{1,0:T(8,128)(2,1)S(1)}, u32[]{:S(2)}, u32[]{:S(2)}) collective-permute-start(bf16[400,256]{1,0:T(8,128)(2,1)S(1)} %collective-permute-done.1.refs_1_), channel_id=1, source_target_pairs={{4,0},{8,4},{12,8},{16,12},{20,16},{24,20},{28,24},{0,28},{5,1},{9... | collective-permute-start | bytes 614408 | tf_op jit(solution)/shard_map/ppermute | solution.py:26
  24.5 0.0 collective-permute-done.3.refs_2_
  24.5 0.0 collective-permute-start.4
  24.5 0.0 collective-permute-done.9
  24.5 2.8 %collective-permute-start.10 = (bf16[400,512]{1,0:T(8,128)(2,1)S(1)}, bf16[400,512]{1,0:T(8,128)(2,1)S(1)}, u32[]{:S(2)}, u32[]{:S(2)}) collective-permute-start(bf16[400,512]{1,0:T(8,128)(2,1)S(1)} %constant_dynamic-update-slice_fusion.2.refs_0_), channel_id=1, source_target_pairs={{64,0},{96,32},{0,64},{32,96},{65,1},{97,33},{1,65},{33,97},{66,2}... | collective-permute-start | bytes 1228808 | tf_op jit(solution)/shard_map/ppermute | solution.py:26
  27.4 0.9 collective-permute-start.11
  28.2 0.0 collective-permute-done.2.refs_3_
  28.2 2.1 %collective-permute-done.4.refs_4_ = bf16[400,256]{1,0:T(8,128)(2,1)S(1)} collective-permute-done((bf16[400,256]{1,0:T(8,128)(2,1)S(1)}, bf16[400,256]{1,0:T(8,128)(2,1)S(1)}, u32[]{:S(2)}, u32[]{:S(2)}) %collective-permute-start.4) | collective-permute-done | bytes 204832 | tf_op jit(solution)/shard_map/ppermute | solution.py:26
  30.3 0.8 select_reduce_fusion
  31.1 0.1 broadcast_in_dim.37
  31.2 0.1 broadcast_in_dim.38
  31.3 1.1 convolution_convert_fusion
  32.4 0.7 collective-permute-start.5
  33.1 0.9 collective-permute-start.6
  33.9 0.9 convolution_convert_fusion.1
  34.8 2.5 %collective-permute-done.5.refs_5_ = bf16[400,256]{1,0:T(8,128)(2,1)S(1)} collective-permute-done((bf16[400,256]{1,0:T(8,128)(2,1)S(1)}, bf16[400,256]{1,0:T(8,128)(2,1)S(1)}, u32[]{:S(2)}, u32[]{:S(2)}) %collective-permute-start.5) | collective-permute-done | bytes 204832 | tf_op jit(solution)/shard_map/ppermute | solution.py:26
  37.4 1.2 %collective-permute-start.12 = (bf16[400,512]{1,0:T(8,128)(2,1)S(1)}, bf16[400,512]{1,0:T(8,128)(2,1)S(1)}, u32[]{:S(2)}, u32[]{:S(2)}) collective-permute-start(bf16[400,512]{1,0:T(8,128)(2,1)S(1)} %constant_dynamic-update-slice_fusion.2.refs_0_), channel_id=1, source_target_pairs={{96,0},{0,32},{32,64},{64,96},{97,1},{1,33},{33,65},{65,97},{98,2}... | collective-permute-start | bytes 1228808 | tf_op jit(solution)/shard_map/ppermute | solution.py:26
  38.6 0.3 collective-permute-done.6.refs_6_
  38.9 1.1 collective-permute-start.7
  39.9 0.9 convolution_convert_fusion.2
  40.9 0.1 broadcast_in_dim.39.dpos
  40.9 0.7 early.1.state
  41.6 2.2 %collective-permute-done.7.refs_7_ = bf16[400,256]{1,0:T(8,128)(2,1)S(1)} collective-permute-done((bf16[400,256]{1,0:T(8,128)(2,1)S(1)}, bf16[400,256]{1,0:T(8,128)(2,1)S(1)}, u32[]{:S(2)}, u32[]{:S(2)}) %collective-permute-start.7) | collective-permute-done | bytes 204832 | tf_op jit(solution)/shard_map/ppermute | solution.py:26
  43.8 1.4 %gather.1 = (bf16[3072,256]{1,0:T(8,128)(2,1)S(1)}, s32[16]{0:T(128)S(1)}, f32[8,8,768]{2,1,0:T(8,128)S(1)}) custom-call(bf16[32,128]{1,0:T(8,128)(2,1)S(1)} %reshape.16.dq, f32[96,128]{1,0:T(8,128)S(1)} %early.1.state, s32[32,128]{1,0:T(8,128)S(1)} %broadcast_in_dim.39.dpos, bf16[400,256]{1,0:T(8,128)(2,1)S(1)} %constant_dynamic-update-slice_fusion.refs_0_, ...), custom_call_target="tpu_custom_call" | custom-call | tf_op jit(solution)/shard_map/gather/pallas_call | solution.py:173
  45.2 0.0 collective-permute-done.8.source
  45.2 3.5 %fetch.1.other_w = bf16[1024,4096]{1,0:T(8,128)(2,1)S(1)} custom-call(bf16[1024,4096]{1,0:T(8,128)(2,1)} %collective-permute-done.8.source), custom_call_target="tpu_custom_call" | custom-call | tf_op jit(solution)/shard_map/fetch/pallas_call | solution.py:408
  48.7 0.0 collective-permute-done.10.refs_0_
  48.7 0.0 slice-start
  48.7 5.7 %attend.3 = bf16[2,136,768]{2,1,0:T(8,128)(2,1)S(1)} custom-call(s32[16]{0:T(128)S(1)} %get-tuple-element.55.table, bf16[400,512]{1,0:T(8,128)(2,1)S(1)} %collective-permute-done.10.refs_0_, bf16[3072,256]{1,0:T(8,128)(2,1)S(1)} %get-tuple-element.50.refs_1_.refs_2_, f32[8,8,768]{2,1,0:T(8,128)S(1)} %get-tuple-element.51.refs_2_.refs_3_), custom_call_target="tpu_custom_call" | custom-call | flops 2415919104 | bytes 4194304 | tf_op jit(solution)/shard_map/attend/pallas_call | solution.py:330
  54.4 0.0 slice-start.1
  54.4 0.0 collective-permute-done.11.refs_0_
  54.5 0.0 collective-permute-done.12.refs_1_
  54.5 7.6 %attend.4 = (bf16[2,136,768]{2,1,0:T(8,128)(2,1)S(1)}, bf16[2,136,768]{2,1,0:T(8,128)(2,1)S(1)}) custom-call(s32[16]{0:T(128)S(1)} %get-tuple-element.55.table, bf16[400,512]{1,0:T(8,128)(2,1)S(1)} %collective-permute-done.11.refs_0_, bf16[400,512]{1,0:T(8,128)(2,1)S(1)} %collective-permute-done.12.refs_1_, ...), custom_call_target="tpu_custom_call" | custom-call | flops 4831838208 | bytes 4194304 | tf_op jit(solution)/shard_map/attend/pallas_call | solution.py:330
  62.1 3.7 %collective-permute-start.13 = (bf16[2,136,768]{2,1,0:T(8,128)(2,1)S(1)}, bf16[2,136,768]{2,1,0:T(8,128)(2,1)S(1)}, u32[]{:S(2)}, u32[]{:S(2)}) collective-permute-start(bf16[2,136,768]{2,1,0:T(8,128)(2,1)S(1)} %get-tuple-element.56), channel_id=1, source_target_pairs={{96,0},{0,32},{32,64},{64,96},{97,1},{1,33},{33,65},{65,97},{98,2}... | collective-permute-start | bytes 1253384 | tf_op jit(solution)/shard_map/ppermute | solution.py:26
  65.8 0.0 collective-permute-start.15
  65.8 1.9 %collective-permute-start.14 = (bf16[2,136,768]{2,1,0:T(8,128)(2,1)S(1)}, bf16[2,136,768]{2,1,0:T(8,128)(2,1)S(1)}, u32[]{:S(2)}, u32[]{:S(2)}) collective-permute-start(bf16[2,136,768]{2,1,0:T(8,128)(2,1)S(1)} %attend.3), channel_id=1, source_target_pairs={{64,0},{96,32},{0,64},{32,96},{65,1},{97,33},{1,65},{33,97},{66,2}... | collective-permute-start | bytes 1253384 | tf_op jit(solution)/shard_map/ppermute | solution.py:26
  67.6 5.9 %attend.5.refs_0_ = bf16[2,136,768]{2,1,0:T(8,128)(2,1)S(1)} custom-call(s32[16]{0:T(128)S(1)} %get-tuple-element.55.table, bf16[400,512]{1,0:T(8,128)(2,1)S(1)} %constant_dynamic-update-slice_fusion.2.refs_0_, bf16[3072,256]{1,0:T(8,128)(2,1)S(1)} %get-tuple-element.50.refs_1_.refs_2_, f32[8,8,768]{2,1,0:T(8,128)S(1)} %get-tuple-element.51.refs_2_.refs_3_), custom_call_target="tpu_custom_call" | custom-call | flops 2415919104 | bytes 4194304 | tf_op jit(solution)/shard_map/attend/pallas_call | solution.py:330
  73.6 0.0 collective-permute-done.13.refs_1_
  73.6 6.4 %collective-permute-done.14.refs_2_ = bf16[2,136,768]{2,1,0:T(8,128)(2,1)S(1)} collective-permute-done((bf16[2,136,768]{2,1,0:T(8,128)(2,1)S(1)}, bf16[2,136,768]{2,1,0:T(8,128)(2,1)S(1)}, u32[]{:S(2)}, u32[]{:S(2)}) %collective-permute-start.14) | collective-permute-done | bytes 417824 | tf_op jit(solution)/shard_map/ppermute | solution.py:26
  80.0 0.7 merge.1
  80.7 3.0 %collective-permute-start.16 = (bf16[104,512]{1,0:T(8,128)(2,1)S(1)}, bf16[104,512]{1,0:T(8,128)(2,1)S(1)}, u32[]{:S(2)}, u32[]{:S(2)}) collective-permute-start(bf16[104,512]{1,0:T(8,128)(2,1)S(1)} %get-tuple-element.60), channel_id=1, source_target_pairs={{128,0},{0,128},{129,1},{1,129},{130,2},{2,130},{131,3},{3,131},{1... | collective-permute-start | bytes 319496 | tf_op jit(solution)/shard_map/ppermute | solution.py:26
  83.7 6.1 %collective-permute-start.17 = (bf16[104,512]{1,0:T(8,128)(2,1)S(1)}, bf16[104,512]{1,0:T(8,128)(2,1)S(1)}, u32[]{:S(2)}, u32[]{:S(2)}) collective-permute-start(bf16[104,512]{1,0:T(8,128)(2,1)S(1)} %get-tuple-element.61), channel_id=1, source_target_pairs={{1,0},{0,1},{3,2},{2,3},{5,4},{4,5},{7,6},{6,7},{9,8},{8,9},{11,10... | collective-permute-start | bytes 319496 | tf_op jit(solution)/shard_map/ppermute | solution.py:26
  89.7 0.0 collective-permute-done.16.by_pair
  89.7 0.9 collective-permute-done.17.by_core
  90.7 5.1 %collective-permute-done.18.by_both = bf16[104,512]{1,0:T(8,128)(2,1)S(1)} collective-permute-done((bf16[104,512]{1,0:T(8,128)(2,1)S(1)}, bf16[104,512]{1,0:T(8,128)(2,1)S(1)}, u32[]{:S(2)}, u32[]{:S(2)}) %collective-permute-start.18) | collective-permute-done | bytes 106528 | tf_op jit(solution)/shard_map/ppermute | solution.py:540
  95.8 1.4 %project.2 = (bf16[48,2048]{1,0:T(8,128)(2,1)S(1)}, f32[56,2048]{1,0:T(8,128)S(1)}) custom-call(bf16[104,512]{1,0:T(8,128)(2,1)S(1)} %get-tuple-element.67.mine, bf16[104,512]{1,0:T(8,128)(2,1)S(1)} %collective-permute-done.16.by_pair, bf16[104,512]{1,0:T(8,128)(2,1)S(1)} %collective-permute-done.17.by_core, ...), custom_call_target="tpu_custom_call" | custom-call | flops 872415232 | bytes 9437184 | tf_op jit(solution)/shard_map/project/pallas_call | solution.py:448
  97.3 1.5 %project.3 = (bf16[48,2176]{1,0:T(8,128)(2,1)S(1)}, f32[56,2048]{1,0:T(8,128)S(1)}) custom-call(bf16[104,512]{1,0:T(8,128)(2,1)S(1)} %get-tuple-element.67.mine, bf16[104,512]{1,0:T(8,128)(2,1)S(1)} %collective-permute-done.16.by_pair, bf16[104,512]{1,0:T(8,128)(2,1)S(1)} %collective-permute-done.17.by_core, ...), custom_call_target="tpu_custom_call" | custom-call | flops 872415232 | bytes 9437184 | tf_op jit(solution)/shard_map/project/pallas_call | solution.py:448
  98.8 0.5 collective-permute-start.20
  99.3 1.1 collective-permute-start.19
  100.3 9.5 %collective-permute-done.19.arrived_0 = bf16[48,2048]{1,0:T(8,128)(2,1)S(1)} collective-permute-done((bf16[48,2048]{1,0:T(8,128)(2,1)S(1)}, bf16[48,2048]{1,0:T(8,128)(2,1)S(1)}, u32[]{:S(2)}, u32[]{:S(2)}) %collective-permute-start.19) | collective-permute-done | bytes 196640 | tf_op jit(solution)/shard_map/ppermute | solution.py:26
  109.8 0.0 collective-permute-done.20.arrived_1
  109.8 0.8 close.1
  (15 shorter events, 0.1 us)
Async XLA Ops:
  0.6 44.5 %collective-permute-start.8 = (bf16[1024,4096]{1,0:T(8,128)(2,1)}, bf16[1024,4096]{1,0:T(8,128)(2,1)}, u32[]{:S(2)}, u32[]{:S(2)}) collective-permute-start(bf16[1024,4096]{1,0:T(8,128)(2,1)} %w.3), channel_id=1, source_target_pairs={{1,0},{0,1},{3,2},{2,3},{5,4},{4,5},{7,6},{6,7},{9,8},{8,9},{11,10... | collective-permute-start | bytes 25165832 | tf_op jit(solution)/shard_map/ppermute | solution.py:26
  4.6 1.0 copy-start
  5.6 0.9 copy-start.1
  6.5 0.9 copy-start.2
  7.5 6.0 %collective-permute-start = (bf16[200,256]{1,0:T(8,128)(2,1)S(1)}, bf16[200,256]{1,0:T(8,128)(2,1)S(1)}, u32[]{:S(2)}, u32[]{:S(2)}) collective-permute-start(bf16[200,256]{1,0:T(8,128)(2,1)S(1)} %get-tuple-element.39), channel_id=1, source_target_pairs={{128,0},{0,128},{129,1},{1,129},{130,2},{2,130},{131,3},{3,131},{1... | collective-permute-start | bytes 307208 | tf_op jit(solution)/shard_map/ppermute | solution.py:26
  13.6 7.5 %collective-permute-start.1 = (bf16[400,256]{1,0:T(8,128)(2,1)S(1)}, bf16[400,256]{1,0:T(8,128)(2,1)S(1)}, u32[]{:S(2)}, u32[]{:S(2)}) collective-permute-start(bf16[400,256]{1,0:T(8,128)(2,1)S(1)} %constant_dynamic-update-slice_fusion.refs_0_), channel_id=1, source_target_pairs={{4,0},{8,4},{12,8},{16,12},{20,16},{24,20},{28,24},{0,28},{5,1},{9... | collective-permute-start | bytes 614408 | tf_op jit(solution)/shard_map/ppermute | solution.py:26
  17.5 7.0 %collective-permute-start.3 = (bf16[400,256]{1,0:T(8,128)(2,1)S(1)}, bf16[400,256]{1,0:T(8,128)(2,1)S(1)}, u32[]{:S(2)}, u32[]{:S(2)}) collective-permute-start(bf16[400,256]{1,0:T(8,128)(2,1)S(1)} %constant_dynamic-update-slice_fusion.refs_0_), channel_id=1, source_target_pairs={{28,0},{0,4},{4,8},{8,12},{12,16},{16,20},{20,24},{24,28},{29,1},{... | collective-permute-start | bytes 614408 | tf_op jit(solution)/shard_map/ppermute | solution.py:26
  17.5 7.0 %collective-permute-start.9 = (bf16[200,512]{1,0:T(8,128)(2,1)S(1)}, bf16[200,512]{1,0:T(8,128)(2,1)S(1)}, u32[]{:S(2)}, u32[]{:S(2)}) collective-permute-start(bf16[200,512]{1,0:T(8,128)(2,1)S(1)} %get-tuple-element.49), channel_id=1, source_target_pairs={{128,0},{0,128},{129,1},{1,129},{130,2},{2,130},{131,3},{3,131},{1... | collective-permute-start | bytes 614408 | tf_op jit(solution)/shard_map/ppermute | solution.py:26
  21.1 7.2 %collective-permute-start.2 = (bf16[400,256]{1,0:T(8,128)(2,1)S(1)}, bf16[400,256]{1,0:T(8,128)(2,1)S(1)}, u32[]{:S(2)}, u32[]{:S(2)}) collective-permute-start(bf16[400,256]{1,0:T(8,128)(2,1)S(1)} %collective-permute-done.1.refs_1_), channel_id=1, source_target_pairs={{4,0},{8,4},{12,8},{16,12},{20,16},{24,20},{28,24},{0,28},{5,1},{9... | collective-permute-start | bytes 614408 | tf_op jit(solution)/shard_map/ppermute | solution.py:26
  24.5 5.8 %collective-permute-start.4 = (bf16[400,256]{1,0:T(8,128)(2,1)S(1)}, bf16[400,256]{1,0:T(8,128)(2,1)S(1)}, u32[]{:S(2)}, u32[]{:S(2)}) collective-permute-start(bf16[400,256]{1,0:T(8,128)(2,1)S(1)} %collective-permute-done.3.refs_2_), channel_id=1, source_target_pairs={{28,0},{0,4},{4,8},{8,12},{12,16},{16,20},{20,24},{24,28},{29,1},{... | collective-permute-start | bytes 614408 | tf_op jit(solution)/shard_map/ppermute | solution.py:26
  24.5 24.1 %collective-permute-start.10 = (bf16[400,512]{1,0:T(8,128)(2,1)S(1)}, bf16[400,512]{1,0:T(8,128)(2,1)S(1)}, u32[]{:S(2)}, u32[]{:S(2)}) collective-permute-start(bf16[400,512]{1,0:T(8,128)(2,1)S(1)} %constant_dynamic-update-slice_fusion.2.refs_0_), channel_id=1, source_target_pairs={{64,0},{96,32},{0,64},{32,96},{65,1},{97,33},{1,65},{33,97},{66,2}... | collective-permute-start | bytes 1228808 | tf_op jit(solution)/shard_map/ppermute | solution.py:26
  27.4 27.1 %collective-permute-start.11 = (bf16[400,512]{1,0:T(8,128)(2,1)S(1)}, bf16[400,512]{1,0:T(8,128)(2,1)S(1)}, u32[]{:S(2)}, u32[]{:S(2)}) collective-permute-start(bf16[400,512]{1,0:T(8,128)(2,1)S(1)} %constant_dynamic-update-slice_fusion.2.refs_0_), channel_id=1, source_target_pairs={{32,0},{64,32},{96,64},{0,96},{33,1},{65,33},{97,65},{1,97},{34,2}... | collective-permute-start | bytes 1228808 | tf_op jit(solution)/shard_map/ppermute | solution.py:26
  32.4 5.0 %collective-permute-start.5 = (bf16[400,256]{1,0:T(8,128)(2,1)S(1)}, bf16[400,256]{1,0:T(8,128)(2,1)S(1)}, u32[]{:S(2)}, u32[]{:S(2)}) collective-permute-start(bf16[400,256]{1,0:T(8,128)(2,1)S(1)} %collective-permute-done.2.refs_3_), channel_id=1, source_target_pairs={{4,0},{8,4},{12,8},{16,12},{20,16},{24,20},{28,24},{0,28},{5,1},{9... | collective-permute-start | bytes 614408 | tf_op jit(solution)/shard_map/ppermute | solution.py:26
  33.1 5.8 %collective-permute-start.6 = (bf16[400,256]{1,0:T(8,128)(2,1)S(1)}, bf16[400,256]{1,0:T(8,128)(2,1)S(1)}, u32[]{:S(2)}, u32[]{:S(2)}) collective-permute-start(bf16[400,256]{1,0:T(8,128)(2,1)S(1)} %collective-permute-done.4.refs_4_), channel_id=1, source_target_pairs={{28,0},{0,4},{4,8},{8,12},{12,16},{16,20},{20,24},{24,28},{29,1},{... | collective-permute-start | bytes 614408 | tf_op jit(solution)/shard_map/ppermute | solution.py:26
  37.4 17.1 %collective-permute-start.12 = (bf16[400,512]{1,0:T(8,128)(2,1)S(1)}, bf16[400,512]{1,0:T(8,128)(2,1)S(1)}, u32[]{:S(2)}, u32[]{:S(2)}) collective-permute-start(bf16[400,512]{1,0:T(8,128)(2,1)S(1)} %constant_dynamic-update-slice_fusion.2.refs_0_), channel_id=1, source_target_pairs={{96,0},{0,32},{32,64},{64,96},{97,1},{1,33},{33,65},{65,97},{98,2}... | collective-permute-start | bytes 1228808 | tf_op jit(solution)/shard_map/ppermute | solution.py:26
  38.9 4.9 %collective-permute-start.7 = (bf16[400,256]{1,0:T(8,128)(2,1)S(1)}, bf16[400,256]{1,0:T(8,128)(2,1)S(1)}, u32[]{:S(2)}, u32[]{:S(2)}) collective-permute-start(bf16[400,256]{1,0:T(8,128)(2,1)S(1)} %collective-permute-done.5.refs_5_), channel_id=1, source_target_pairs={{4,0},{8,4},{12,8},{16,12},{20,16},{24,20},{28,24},{0,28},{5,1},{9... | collective-permute-start | bytes 614408 | tf_op jit(solution)/shard_map/ppermute | solution.py:26
  48.7 47.2 %slice-start = ((s8[8388608]{0:T(1024)(128)(4,1)}), s8[4194304]{0:T(1024)(128)(4,1)S(1)}, s32[]{:S(2)}) async-start(s8[8388608]{0:T(1024)(128)(4,1)} %bitcast.10), calls=%async_computation | async-start | bytes 8388608
  54.4 41.4 %slice-start.1 = ((s8[8388608]{0:T(1024)(128)(4,1)}), s8[4194304]{0:T(1024)(128)(4,1)S(1)}, s32[]{:S(2)}) async-start(s8[8388608]{0:T(1024)(128)(4,1)} %bitcast.10), calls=%async_computation.1 | async-start | bytes 8388608
  62.1 11.5 %collective-permute-start.13 = (bf16[2,136,768]{2,1,0:T(8,128)(2,1)S(1)}, bf16[2,136,768]{2,1,0:T(8,128)(2,1)S(1)}, u32[]{:S(2)}, u32[]{:S(2)}) collective-permute-start(bf16[2,136,768]{2,1,0:T(8,128)(2,1)S(1)} %get-tuple-element.56), channel_id=1, source_target_pairs={{96,0},{0,32},{32,64},{64,96},{97,1},{1,33},{33,65},{65,97},{98,2}... | collective-permute-start | bytes 1253384 | tf_op jit(solution)/shard_map/ppermute | solution.py:26
  65.8 7.8 %collective-permute-start.15 = (bf16[2,136,768]{2,1,0:T(8,128)(2,1)S(1)}, bf16[2,136,768]{2,1,0:T(8,128)(2,1)S(1)}, u32[]{:S(2)}, u32[]{:S(2)}) collective-permute-start(bf16[2,136,768]{2,1,0:T(8,128)(2,1)S(1)} %get-tuple-element.58), channel_id=1, source_target_pairs={{32,0},{64,32},{96,64},{0,96},{33,1},{65,33},{97,65},{1,97},{34,2}... | collective-permute-start | bytes 1253384 | tf_op jit(solution)/shard_map/ppermute | solution.py:26
  65.8 14.2 %collective-permute-start.14 = (bf16[2,136,768]{2,1,0:T(8,128)(2,1)S(1)}, bf16[2,136,768]{2,1,0:T(8,128)(2,1)S(1)}, u32[]{:S(2)}, u32[]{:S(2)}) collective-permute-start(bf16[2,136,768]{2,1,0:T(8,128)(2,1)S(1)} %attend.3), channel_id=1, source_target_pairs={{64,0},{96,32},{0,64},{32,96},{65,1},{97,33},{1,65},{33,97},{66,2}... | collective-permute-start | bytes 1253384 | tf_op jit(solution)/shard_map/ppermute | solution.py:26
  80.7 9.1 %collective-permute-start.16 = (bf16[104,512]{1,0:T(8,128)(2,1)S(1)}, bf16[104,512]{1,0:T(8,128)(2,1)S(1)}, u32[]{:S(2)}, u32[]{:S(2)}) collective-permute-start(bf16[104,512]{1,0:T(8,128)(2,1)S(1)} %get-tuple-element.60), channel_id=1, source_target_pairs={{128,0},{0,128},{129,1},{1,129},{130,2},{2,130},{131,3},{3,131},{1... | collective-permute-start | bytes 319496 | tf_op jit(solution)/shard_map/ppermute | solution.py:26
  83.7 7.0 %collective-permute-start.17 = (bf16[104,512]{1,0:T(8,128)(2,1)S(1)}, bf16[104,512]{1,0:T(8,128)(2,1)S(1)}, u32[]{:S(2)}, u32[]{:S(2)}) collective-permute-start(bf16[104,512]{1,0:T(8,128)(2,1)S(1)} %get-tuple-element.61), channel_id=1, source_target_pairs={{1,0},{0,1},{3,2},{2,3},{5,4},{4,5},{7,6},{6,7},{9,8},{8,9},{11,10... | collective-permute-start | bytes 319496 | tf_op jit(solution)/shard_map/ppermute | solution.py:26
  89.7 6.1 %collective-permute-start.18 = (bf16[104,512]{1,0:T(8,128)(2,1)S(1)}, bf16[104,512]{1,0:T(8,128)(2,1)S(1)}, u32[]{:S(2)}, u32[]{:S(2)}) collective-permute-start(bf16[104,512]{1,0:T(8,128)(2,1)S(1)} %get-tuple-element.62), channel_id=1, source_target_pairs={{0,129},{1,128},{128,1},{129,0},{2,131},{3,130},{130,3},{131,2},{4... | collective-permute-start | bytes 319496 | tf_op jit(solution)/shard_map/ppermute | solution.py:540
  98.8 11.0 %collective-permute-start.20 = (bf16[48,2176]{1,0:T(8,128)(2,1)S(1)}, bf16[48,2176]{1,0:T(8,128)(2,1)S(1)}, u32[]{:S(2)}, u32[]{:S(2)}) collective-permute-start(bf16[48,2176]{1,0:T(8,128)(2,1)S(1)} %get-tuple-element.73), channel_id=1, source_target_pairs={{2,0},{0,2},{3,1},{1,3},{6,4},{4,6},{7,5},{5,7},{10,8},{8,10},{11,... | collective-permute-start | bytes 626696 | tf_op jit(solution)/shard_map/ppermute | solution.py:26
  99.3 10.5 %collective-permute-start.19 = (bf16[48,2048]{1,0:T(8,128)(2,1)S(1)}, bf16[48,2048]{1,0:T(8,128)(2,1)S(1)}, u32[]{:S(2)}, u32[]{:S(2)}) collective-permute-start(bf16[48,2048]{1,0:T(8,128)(2,1)S(1)} %get-tuple-element.72), channel_id=1, source_target_pairs={{2,0},{0,2},{3,1},{1,3},{6,4},{4,6},{7,5},{5,7},{10,8},{8,10},{11,... | collective-permute-start | bytes 589832 | tf_op jit(solution)/shard_map/ppermute | solution.py:26

commit v2 on v1

--- a/solution.py
+++ b/solution.py
@@ -38,43 +38,42 @@
     return pltpu.CompilerParams(vmem_limit_bytes=24 << 20)
 
 
-def pack_body(offset, q, k, v, kv_mine, kv_other, q_mine, q_other, sems):
+def pack_body(offset, *refs):
+    arrays, (mine, other, sems) = refs[:-3], refs[-3:]
+    count = len(arrays)
     yh = lax.axis_index("yh")
+    width = mine.shape[1] // count
     copies = []
-
-    def copy(source, width, head, target, at):
+    for target, head in ((other, 1 - yh), (mine, yh)):
         cols = pl.ds(pl.multiple_of(head * width, width), width)
-        copies.append(
-            pltpu.make_async_copy(
-                source.at[:, cols], target.at[0:T, at : at + width], sems.at[len(copies)]
+        for n, a in enumerate(arrays):
+            copies.append(
+                pltpu.make_async_copy(
+                    a.at[:, cols],
+                    target.at[0:T, n * width : (n + 1) * width],
+                    sems.at[len(copies)],
+                )
             )
-        )
-        copies[-1].start()
-
-    for kv, qq, head in ((kv_other, q_other, 1 - yh), (kv_mine, q_mine, yh)):
-        copy(k, HEAD_SIZE, head, kv, 0)
-        copy(v, HEAD_SIZE, head, kv, HEAD_SIZE)
-        copy(q, 512, head, qq, 0)
-    tile = jnp.full((8, 512), offset[0], jnp.int32).astype(jnp.float32).astype(jnp.bfloat16)
-    for kv, qq in ((kv_mine, q_mine), (kv_other, q_other)):
-        kv[T:TP, :] = tile[:, :256]
-        qq[T:TP, :] = tile
+            copies[-1].start()
+    tile = jnp.full((8, mine.shape[1]), offset[0], jnp.int32)
+    tile = tile.astype(jnp.float32).astype(jnp.bfloat16)
+    for target in (mine, other):
+        target[T:TP, :] = tile
     for c in copies:
         c.wait()
 
 
-def pack(offset, q, k, v):
+def pack(offset, *arrays):
+    width = sum(a.shape[1] for a in arrays) // 2
     return pl.pallas_call(
         pack_body,
-        in_specs=[spec(pltpu.SMEM)] + [spec(pltpu.HBM)] * 3,
-        out_specs=[spec()] * 4,
-        out_shape=[
-            jax.ShapeDtypeStruct((TP, width), jnp.bfloat16) for width in (256, 256, 512, 512)
-        ],
-        scratch_shapes=[pltpu.SemaphoreType.DMA((6,))],
+        in_specs=[spec(pltpu.SMEM)] + [spec(pltpu.HBM)] * len(arrays),
+        out_specs=[spec()] * 2,
+        out_shape=[jax.ShapeDtypeStruct((TP, width), jnp.bfloat16)] * 2,
+        scratch_shapes=[pltpu.SemaphoreType.DMA((2 * len(arrays),))],
         compiler_params=params(),
         name="pack",
-    )(offset, q, k, v)
+    )(offset, *arrays)
 
 
 def dec_step(q, blocks, acc, top, total):
@@ -488,7 +487,8 @@
 
 def layer(q, k, v, span_offset, appended_q, appended_k, appended_v, dec_pos, out_weight):
     yh, x, z = (lax.axis_index(a) for a in ("yh", "x", "z"))
-    kv_mine, kv_other, q_mine, q_other = pack(span_offset, q, k, v)
+    kv_mine, kv_other = pack(span_offset, k, v)
+    q_mine, q_other = pack(span_offset, q)
     kv_pair = jnp.concatenate([kv_mine, shift(kv_other, "yh", 1)], axis=0)
     q_pair = jnp.concatenate([q_mine, shift(q_other, "yh", 1)], axis=0)
 
@@ -524,7 +524,6 @@
     f3, b3 = shift(f2, "z", 1), shift(b2, "z", -1)
     f4 = shift(f3, "z", 1)
     kv, table, dec = gather(6, [dq, state, dpos], [kv_pair, f1, b1, f2, b2, f3, b3, f4])
-    table, other_weight = lax.optimization_barrier((table, other_weight))
     (far,) = attend_call(table, [groups[2]], kv, dec, [2])
     table, far = lax.optimization_barrier((table, far))
     back2 = shift(far, "x", 2)

time: 112 us -> 110 us (0.982)
  the two profiles are of different devices: /device:TPU:1 before, /device:TPU:70 now
where the time goes in v2:
time: 110 us
  waiting for transfers between devices  36.6 us (33%)
  starting transfers between devices  35.6 us (32%)
  Pallas kernels  29.3 us (27%)
  local copies, waits for them, and re-layouts  3.17 us (3%)
  matrix products  2.9 us (3%)
  between operations  1.46 us (1%)
    ppermute x20, starting transfers between devices, shift(): return lax.ppermute(x, axis, [((i + k) % n, i) for i in range(n)])  35.2 us
    ppermute x20, waiting for transfers between devices, shift(): return lax.ppermute(x, axis, [((i + k) % n, i) for i in range(n)])  34.7 us
    pallas_call x3, Pallas kernels, attend_call(): pl.pallas_call(partial(attend_body, groups), in_specs=[spec(pltpu.SMEM)]...  19.1 us
    pallas_call x1, Pallas kernels, fetch(): pl.pallas_call(fetch_body, in_specs=[spec(pltpu.HBM)], out_specs=spec(),...  3.68 us
    pallas_call x2, Pallas kernels, project(): pl.pallas_call(partial(project_body, half), in_specs=[spec()] * len(opera...  2.92 us
    dot_general x3, matrix products, rows_of(): jnp.dot(pick, a, preferred_element_type=jnp.float32).astype(jnp.bfloat16)  2.9 us
    unnamed x12, local copies, waits for them, and re-layouts  2.8 us
  transfers between devices with their start and end apart: 21, of which 11 were waited for; matrix products, arithmetic and copies ran while one was open for 4% of the time, Pallas kernels for 23%

profile of v2, /device:TPU:70, one launch (start us, length us, event | category | flops | bytes accessed | tf_op | source)
XLA Modules:
  0.0 110.0 jit_solution(14944339803504746707)
XLA Ops:
  0.6 0.1 collective-permute-start.18
  1.4 0.9 copy-done.1
  2.3 0.9 copy-done.2
  3.2 0.1 pack.2
  3.3 3.3 %collective-permute-start = (bf16[200,256]{1,0:T(8,128)(2,1)S(1)}, bf16[200,256]{1,0:T(8,128)(2,1)S(1)}, u32[]{:S(2)}, u32[]{:S(2)}) collective-permute-start(bf16[200,256]{1,0:T(8,128)(2,1)S(1)} %get-tuple-element.37), channel_id=1, source_target_pairs={{128,0},{0,128},{129,1},{1,129},{130,2},{2,130},{131,3},{3,131},{1... | collective-permute-start | bytes 307208 | tf_op jit(solution)/shard_map/ppermute | solution.py:26
  6.5 3.6 %collective-permute-done = bf16[200,256]{1,0:T(8,128)(2,1)S(1)} collective-permute-done((bf16[200,256]{1,0:T(8,128)(2,1)S(1)}, bf16[200,256]{1,0:T(8,128)(2,1)S(1)}, u32[]{:S(2)}, u32[]{:S(2)}) %collective-permute-start) | collective-permute-done | bytes 102432 | tf_op jit(solution)/shard_map/ppermute | solution.py:26
  10.1 2.0 %collective-permute-start.3 = (bf16[400,256]{1,0:T(8,128)(2,1)S(1)}, bf16[400,256]{1,0:T(8,128)(2,1)S(1)}, u32[]{:S(2)}, u32[]{:S(2)}) collective-permute-start(bf16[400,256]{1,0:T(8,128)(2,1)S(1)} %constant_dynamic-update-slice_fusion.refs_0_), channel_id=1, source_target_pairs={{28,0},{0,4},{4,8},{8,12},{12,16},{16,20},{20,24},{24,28},{29,1},{... | collective-permute-start | bytes 614408 | tf_op jit(solution)/shard_map/ppermute | solution.py:26
  12.1 0.1 collective-permute-start.1
  12.3 1.0 copy-done
  13.2 0.1 pack.3
  13.3 3.3 %collective-permute-start.8 = (bf16[200,512]{1,0:T(8,128)(2,1)S(1)}, bf16[200,512]{1,0:T(8,128)(2,1)S(1)}, u32[]{:S(2)}, u32[]{:S(2)}) collective-permute-start(bf16[200,512]{1,0:T(8,128)(2,1)S(1)} %get-tuple-element.46), channel_id=1, source_target_pairs={{128,0},{0,128},{129,1},{1,129},{130,2},{2,130},{131,3},{3,131},{1... | collective-permute-start | bytes 614408 | tf_op jit(solution)/shard_map/ppermute | solution.py:26
  16.6 0.1 stack.35
  16.7 0.1 collective-permute-done.3.refs_2_
  16.9 3.0 %collective-permute-start.4 = (bf16[400,256]{1,0:T(8,128)(2,1)S(1)}, bf16[400,256]{1,0:T(8,128)(2,1)S(1)}, u32[]{:S(2)}, u32[]{:S(2)}) collective-permute-start(bf16[400,256]{1,0:T(8,128)(2,1)S(1)} %collective-permute-done.3.refs_2_), channel_id=1, source_target_pairs={{28,0},{0,4},{4,8},{8,12},{12,16},{16,20},{20,24},{24,28},{29,1},{... | collective-permute-start | bytes 614408 | tf_op jit(solution)/shard_map/ppermute | solution.py:26
  19.8 0.1 collective-permute-done.1.refs_1_
  19.9 0.0 collective-permute-start.2
  19.9 1.3 %collective-permute-done.8 = bf16[200,512]{1,0:T(8,128)(2,1)S(1)} collective-permute-done((bf16[200,512]{1,0:T(8,128)(2,1)S(1)}, bf16[200,512]{1,0:T(8,128)(2,1)S(1)}, u32[]{:S(2)}, u32[]{:S(2)}) %collective-permute-start.8) | collective-permute-done | bytes 204832 | tf_op jit(solution)/shard_map/ppermute | solution.py:26
  21.2 0.6 collective-permute-start.11
  21.7 2.4 %collective-permute-start.9 = (bf16[400,512]{1,0:T(8,128)(2,1)S(1)}, bf16[400,512]{1,0:T(8,128)(2,1)S(1)}, u32[]{:S(2)}, u32[]{:S(2)}) collective-permute-start(bf16[400,512]{1,0:T(8,128)(2,1)S(1)} %constant_dynamic-update-slice_fusion.2.refs_0_), channel_id=1, source_target_pairs={{64,0},{96,32},{0,64},{32,96},{65,1},{97,33},{1,65},{33,97},{66,2}... | collective-permute-start | bytes 1228808 | tf_op jit(solution)/shard_map/ppermute | solution.py:26
  24.2 0.0 collective-permute-done.4.refs_4_
  24.2 2.7 %collective-permute-done.2.refs_3_ = bf16[400,256]{1,0:T(8,128)(2,1)S(1)} collective-permute-done((bf16[400,256]{1,0:T(8,128)(2,1)S(1)}, bf16[400,256]{1,0:T(8,128)(2,1)S(1)}, u32[]{:S(2)}, u32[]{:S(2)}) %collective-permute-start.2) | collective-permute-done | bytes 204832 | tf_op jit(solution)/shard_map/ppermute | solution.py:26
  26.9 0.8 select_reduce_fusion
  27.7 0.1 broadcast_in_dim.37
  27.8 0.1 broadcast_in_dim.38
  27.9 1.1 convolution_convert_fusion
  28.9 0.1 collective-permute-start.5
  29.0 3.3 %collective-permute-start.6 = (bf16[400,256]{1,0:T(8,128)(2,1)S(1)}, bf16[400,256]{1,0:T(8,128)(2,1)S(1)}, u32[]{:S(2)}, u32[]{:S(2)}) collective-permute-start(bf16[400,256]{1,0:T(8,128)(2,1)S(1)} %collective-permute-done.4.refs_4_), channel_id=1, source_target_pairs={{28,0},{0,4},{4,8},{8,12},{12,16},{16,20},{20,24},{24,28},{29,1},{... | collective-permute-start | bytes 614408 | tf_op jit(solution)/shard_map/ppermute | solution.py:26
  32.3 0.9 convolution_convert_fusion.2
  33.2 2.7 %collective-permute-done.5.refs_5_ = bf16[400,256]{1,0:T(8,128)(2,1)S(1)} collective-permute-done((bf16[400,256]{1,0:T(8,128)(2,1)S(1)}, bf16[400,256]{1,0:T(8,128)(2,1)S(1)}, u32[]{:S(2)}, u32[]{:S(2)}) %collective-permute-start.5) | collective-permute-done | bytes 204832 | tf_op jit(solution)/shard_map/ppermute | solution.py:26
  36.0 0.8 collective-permute-start.10
  36.8 0.0 collective-permute-done.6.refs_6_
  36.8 0.5 collective-permute-start.7
  37.3 0.9 convolution_convert_fusion.1
  38.2 0.1 broadcast_in_dim.39.dpos
  38.3 0.7 early.1.state
  39.0 4.8 %collective-permute-done.7.refs_7_ = bf16[400,256]{1,0:T(8,128)(2,1)S(1)} collective-permute-done((bf16[400,256]{1,0:T(8,128)(2,1)S(1)}, bf16[400,256]{1,0:T(8,128)(2,1)S(1)}, u32[]{:S(2)}, u32[]{:S(2)}) %collective-permute-start.7) | collective-permute-done | bytes 204832 | tf_op jit(solution)/shard_map/ppermute | solution.py:26
  43.8 1.4 %gather.1 = (bf16[3072,256]{1,0:T(8,128)(2,1)S(1)}, s32[16]{0:T(128)S(1)}, f32[8,8,768]{2,1,0:T(8,128)S(1)}) custom-call(bf16[32,128]{1,0:T(8,128)(2,1)S(1)} %reshape.16.dq, f32[96,128]{1,0:T(8,128)S(1)} %early.1.state, s32[32,128]{1,0:T(8,128)S(1)} %broadcast_in_dim.39.dpos, bf16[400,256]{1,0:T(8,128)(2,1)S(1)} %constant_dynamic-update-slice_fusion.refs_0_, ...), custom_call_target="tpu_custom_call" | custom-call | tf_op jit(solution)/shard_map/gather/pallas_call | solution.py:172
  45.1 0.0 collective-permute-done.9.refs_0_
  45.2 5.7 %attend.3 = bf16[2,136,768]{2,1,0:T(8,128)(2,1)S(1)} custom-call(s32[16]{0:T(128)S(1)} %get-tuple-element.52.table, bf16[400,512]{1,0:T(8,128)(2,1)S(1)} %collective-permute-done.9.refs_0_, bf16[3072,256]{1,0:T(8,128)(2,1)S(1)} %get-tuple-element.47.refs_1_.refs_2_, f32[8,8,768]{2,1,0:T(8,128)S(1)} %get-tuple-element.48.refs_2_.refs_3_), custom_call_target="tpu_custom_call" | custom-call | flops 2415919104 | bytes 4194304 | tf_op jit(solution)/shard_map/attend/pallas_call | solution.py:329
  50.9 0.0 collective-permute-done.11.refs_1_
  50.9 0.0 collective-permute-done.10.refs_0_
  50.9 7.4 %attend.4 = (bf16[2,136,768]{2,1,0:T(8,128)(2,1)S(1)}, bf16[2,136,768]{2,1,0:T(8,128)(2,1)S(1)}) custom-call(s32[16]{0:T(128)S(1)} %get-tuple-element.52.table, bf16[400,512]{1,0:T(8,128)(2,1)S(1)} %collective-permute-done.10.refs_0_, bf16[400,512]{1,0:T(8,128)(2,1)S(1)} %collective-permute-done.11.refs_1_, ...), custom_call_target="tpu_custom_call" | custom-call | flops 4831838208 | bytes 4194304 | tf_op jit(solution)/shard_map/attend/pallas_call | solution.py:329
  58.3 8.9 %collective-permute-start.12 = (bf16[2,136,768]{2,1,0:T(8,128)(2,1)S(1)}, bf16[2,136,768]{2,1,0:T(8,128)(2,1)S(1)}, u32[]{:S(2)}, u32[]{:S(2)}) collective-permute-start(bf16[2,136,768]{2,1,0:T(8,128)(2,1)S(1)} %get-tuple-element.53), channel_id=1, source_target_pairs={{96,0},{0,32},{32,64},{64,96},{97,1},{1,33},{33,65},{65,97},{98,2}... | collective-permute-start | bytes 1253384 | tf_op jit(solution)/shard_map/ppermute | solution.py:26
  67.2 0.0 collective-permute-start.14
  67.2 1.6 %collective-permute-start.13 = (bf16[2,136,768]{2,1,0:T(8,128)(2,1)S(1)}, bf16[2,136,768]{2,1,0:T(8,128)(2,1)S(1)}, u32[]{:S(2)}, u32[]{:S(2)}) collective-permute-start(bf16[2,136,768]{2,1,0:T(8,128)(2,1)S(1)} %attend.3), channel_id=1, source_target_pairs={{64,0},{96,32},{0,64},{32,96},{65,1},{97,33},{1,65},{33,97},{66,2}... | collective-permute-start | bytes 1253384 | tf_op jit(solution)/shard_map/ppermute | solution.py:26
  68.7 5.9 %attend.5.refs_0_ = bf16[2,136,768]{2,1,0:T(8,128)(2,1)S(1)} custom-call(s32[16]{0:T(128)S(1)} %get-tuple-element.52.table, bf16[400,512]{1,0:T(8,128)(2,1)S(1)} %constant_dynamic-update-slice_fusion.2.refs_0_, bf16[3072,256]{1,0:T(8,128)(2,1)S(1)} %get-tuple-element.47.refs_1_.refs_2_, f32[8,8,768]{2,1,0:T(8,128)S(1)} %get-tuple-element.48.refs_2_.refs_3_), custom_call_target="tpu_custom_call" | custom-call | flops 2415919104 | bytes 4194304 | tf_op jit(solution)/shard_map/attend/pallas_call | solution.py:329
  74.7 6.2 %collective-permute-done.12.refs_1_ = bf16[2,136,768]{2,1,0:T(8,128)(2,1)S(1)} collective-permute-done((bf16[2,136,768]{2,1,0:T(8,128)(2,1)S(1)}, bf16[2,136,768]{2,1,0:T(8,128)(2,1)S(1)}, u32[]{:S(2)}, u32[]{:S(2)}) %collective-permute-start.12) | collective-permute-done | bytes 417824 | tf_op jit(solution)/shard_map/ppermute | solution.py:26
  80.9 3.4 %collective-permute-done.14.refs_3_ = bf16[2,136,768]{2,1,0:T(8,128)(2,1)S(1)} collective-permute-done((bf16[2,136,768]{2,1,0:T(8,128)(2,1)S(1)}, bf16[2,136,768]{2,1,0:T(8,128)(2,1)S(1)}, u32[]{:S(2)}, u32[]{:S(2)}) %collective-permute-start.14) | collective-permute-done | bytes 417824 | tf_op jit(solution)/shard_map/ppermute | solution.py:26
  84.3 0.0 collective-permute-done.13.refs_2_
  84.3 0.7 merge.1
  84.9 3.3 %collective-permute-start.15 = (bf16[104,512]{1,0:T(8,128)(2,1)S(1)}, bf16[104,512]{1,0:T(8,128)(2,1)S(1)}, u32[]{:S(2)}, u32[]{:S(2)}) collective-permute-start(bf16[104,512]{1,0:T(8,128)(2,1)S(1)} %get-tuple-element.57), channel_id=1, source_target_pairs={{128,0},{0,128},{129,1},{1,129},{130,2},{2,130},{131,3},{3,131},{1... | collective-permute-start | bytes 319496 | tf_op jit(solution)/shard_map/ppermute | solution.py:26
  88.2 0.0 collective-permute-start.16
  88.2 0.4 collective-permute-start.17
  88.7 0.0 collective-permute-done.18.source
  88.7 3.7 %fetch.1.other_w = bf16[1024,4096]{1,0:T(8,128)(2,1)S(1)} custom-call(bf16[1024,4096]{1,0:T(8,128)(2,1)} %collective-permute-done.18.source), custom_call_target="tpu_custom_call" | custom-call | tf_op jit(solution)/shard_map/fetch/pallas_call | solution.py:407
  92.4 0.0 collective-permute-done.15.by_pair
  92.4 0.0 collective-permute-done.16.by_core
  92.4 1.9 %collective-permute-done.17.by_both = bf16[104,512]{1,0:T(8,128)(2,1)S(1)} collective-permute-done((bf16[104,512]{1,0:T(8,128)(2,1)S(1)}, bf16[104,512]{1,0:T(8,128)(2,1)S(1)}, u32[]{:S(2)}, u32[]{:S(2)}) %collective-permute-start.17) | collective-permute-done | bytes 106528 | tf_op jit(solution)/shard_map/ppermute | solution.py:539
  94.3 1.4 %project.2 = (bf16[48,2048]{1,0:T(8,128)(2,1)S(1)}, f32[56,2048]{1,0:T(8,128)S(1)}) custom-call(bf16[104,512]{1,0:T(8,128)(2,1)S(1)} %get-tuple-element.63.mine, bf16[104,512]{1,0:T(8,128)(2,1)S(1)} %collective-permute-done.15.by_pair, bf16[104,512]{1,0:T(8,128)(2,1)S(1)} %collective-permute-done.16.by_core, ...), custom_call_target="tpu_custom_call" | custom-call | flops 872415232 | bytes 9437184 | tf_op jit(solution)/shard_map/project/pallas_call | solution.py:447
  95.8 1.5 %project.3 = (bf16[48,2176]{1,0:T(8,128)(2,1)S(1)}, f32[56,2048]{1,0:T(8,128)S(1)}) custom-call(bf16[104,512]{1,0:T(8,128)(2,1)S(1)} %get-tuple-element.63.mine, bf16[104,512]{1,0:T(8,128)(2,1)S(1)} %collective-permute-done.15.by_pair, bf16[104,512]{1,0:T(8,128)(2,1)S(1)} %collective-permute-done.16.by_core, ...), custom_call_target="tpu_custom_call" | custom-call | flops 872415232 | bytes 9437184 | tf_op jit(solution)/shard_map/project/pallas_call | solution.py:447
  97.3 0.8 collective-permute-start.20
  98.0 1.3 %collective-permute-start.19 = (bf16[48,2048]{1,0:T(8,128)(2,1)S(1)}, bf16[48,2048]{1,0:T(8,128)(2,1)S(1)}, u32[]{:S(2)}, u32[]{:S(2)}) collective-permute-start(bf16[48,2048]{1,0:T(8,128)(2,1)S(1)} %get-tuple-element.68), channel_id=1, source_target_pairs={{2,0},{0,2},{3,1},{1,3},{6,4},{4,6},{7,5},{5,7},{10,8},{8,10},{11,... | collective-permute-start | bytes 589832 | tf_op jit(solution)/shard_map/ppermute | solution.py:26
  99.4 9.8 %collective-permute-done.19.arrived_0 = bf16[48,2048]{1,0:T(8,128)(2,1)S(1)} collective-permute-done((bf16[48,2048]{1,0:T(8,128)(2,1)S(1)}, bf16[48,2048]{1,0:T(8,128)(2,1)S(1)}, u32[]{:S(2)}, u32[]{:S(2)}) %collective-permute-start.19) | collective-permute-done | bytes 196640 | tf_op jit(solution)/shard_map/ppermute | solution.py:26
  109.1 0.8 close.1
  (16 shorter events, 0.1 us)
Async XLA Ops:
  0.6 88.0 %collective-permute-start.18 = (bf16[1024,4096]{1,0:T(8,128)(2,1)}, bf16[1024,4096]{1,0:T(8,128)(2,1)}, u32[]{:S(2)}, u32[]{:S(2)}) collective-permute-start(bf16[1024,4096]{1,0:T(8,128)(2,1)} %w.3), channel_id=1, source_target_pairs={{1,0},{0,1},{3,2},{2,3},{5,4},{4,5},{7,6},{6,7},{9,8},{8,9},{11,10... | collective-permute-start | bytes 25165832 | tf_op jit(solution)/shard_map/ppermute | solution.py:26
  1.4 0.9 copy-start.1
  2.3 0.9 copy-start.2
  3.3 6.9 %collective-permute-start = (bf16[200,256]{1,0:T(8,128)(2,1)S(1)}, bf16[200,256]{1,0:T(8,128)(2,1)S(1)}, u32[]{:S(2)}, u32[]{:S(2)}) collective-permute-start(bf16[200,256]{1,0:T(8,128)(2,1)S(1)} %get-tuple-element.37), channel_id=1, source_target_pairs={{128,0},{0,128},{129,1},{1,129},{130,2},{2,130},{131,3},{3,131},{1... | collective-permute-start | bytes 307208 | tf_op jit(solution)/shard_map/ppermute | solution.py:26
  10.1 6.7 %collective-permute-start.3 = (bf16[400,256]{1,0:T(8,128)(2,1)S(1)}, bf16[400,256]{1,0:T(8,128)(2,1)S(1)}, u32[]{:S(2)}, u32[]{:S(2)}) collective-permute-start(bf16[400,256]{1,0:T(8,128)(2,1)S(1)} %constant_dynamic-update-slice_fusion.refs_0_), channel_id=1, source_target_pairs={{28,0},{0,4},{4,8},{8,12},{12,16},{16,20},{20,24},{24,28},{29,1},{... | collective-permute-start | bytes 614408 | tf_op jit(solution)/shard_map/ppermute | solution.py:26
  12.1 7.7 %collective-permute-start.1 = (bf16[400,256]{1,0:T(8,128)(2,1)S(1)}, bf16[400,256]{1,0:T(8,128)(2,1)S(1)}, u32[]{:S(2)}, u32[]{:S(2)}) collective-permute-start(bf16[400,256]{1,0:T(8,128)(2,1)S(1)} %constant_dynamic-update-slice_fusion.refs_0_), channel_id=1, source_target_pairs={{4,0},{8,4},{12,8},{16,12},{20,16},{24,20},{28,24},{0,28},{5,1},{9... | collective-permute-start | bytes 614408 | tf_op jit(solution)/shard_map/ppermute | solution.py:26
  12.3 1.0 copy-start
  13.3 7.8 %collective-permute-start.8 = (bf16[200,512]{1,0:T(8,128)(2,1)S(1)}, bf16[200,512]{1,0:T(8,128)(2,1)S(1)}, u32[]{:S(2)}, u32[]{:S(2)}) collective-permute-start(bf16[200,512]{1,0:T(8,128)(2,1)S(1)} %get-tuple-element.46), channel_id=1, source_target_pairs={{128,0},{0,128},{129,1},{1,129},{130,2},{2,130},{131,3},{3,131},{1... | collective-permute-start | bytes 614408 | tf_op jit(solution)/shard_map/ppermute | solution.py:26
  16.9 7.3 %collective-permute-start.4 = (bf16[400,256]{1,0:T(8,128)(2,1)S(1)}, bf16[400,256]{1,0:T(8,128)(2,1)S(1)}, u32[]{:S(2)}, u32[]{:S(2)}) collective-permute-start(bf16[400,256]{1,0:T(8,128)(2,1)S(1)} %collective-permute-done.3.refs_2_), channel_id=1, source_target_pairs={{28,0},{0,4},{4,8},{8,12},{12,16},{16,20},{20,24},{24,28},{29,1},{... | collective-permute-start | bytes 614408 | tf_op jit(solution)/shard_map/ppermute | solution.py:26
  19.9 7.0 %collective-permute-start.2 = (bf16[400,256]{1,0:T(8,128)(2,1)S(1)}, bf16[400,256]{1,0:T(8,128)(2,1)S(1)}, u32[]{:S(2)}, u32[]{:S(2)}) collective-permute-start(bf16[400,256]{1,0:T(8,128)(2,1)S(1)} %collective-permute-done.1.refs_1_), channel_id=1, source_target_pairs={{4,0},{8,4},{12,8},{16,12},{20,16},{24,20},{28,24},{0,28},{5,1},{9... | collective-permute-start | bytes 614408 | tf_op jit(solution)/shard_map/ppermute | solution.py:26
  21.2 29.7 %collective-permute-start.11 = (bf16[400,512]{1,0:T(8,128)(2,1)S(1)}, bf16[400,512]{1,0:T(8,128)(2,1)S(1)}, u32[]{:S(2)}, u32[]{:S(2)}) collective-permute-start(bf16[400,512]{1,0:T(8,128)(2,1)S(1)} %constant_dynamic-update-slice_fusion.2.refs_0_), channel_id=1, source_target_pairs={{96,0},{0,32},{32,64},{64,96},{97,1},{1,33},{33,65},{65,97},{98,2}... | collective-permute-start | bytes 1228808 | tf_op jit(solution)/shard_map/ppermute | solution.py:26
  21.7 23.4 %collective-permute-start.9 = (bf16[400,512]{1,0:T(8,128)(2,1)S(1)}, bf16[400,512]{1,0:T(8,128)(2,1)S(1)}, u32[]{:S(2)}, u32[]{:S(2)}) collective-permute-start(bf16[400,512]{1,0:T(8,128)(2,1)S(1)} %constant_dynamic-update-slice_fusion.2.refs_0_), channel_id=1, source_target_pairs={{64,0},{96,32},{0,64},{32,96},{65,1},{97,33},{1,65},{33,97},{66,2}... | collective-permute-start | bytes 1228808 | tf_op jit(solution)/shard_map/ppermute | solution.py:26
  28.9 7.0 %collective-permute-start.5 = (bf16[400,256]{1,0:T(8,128)(2,1)S(1)}, bf16[400,256]{1,0:T(8,128)(2,1)S(1)}, u32[]{:S(2)}, u32[]{:S(2)}) collective-permute-start(bf16[400,256]{1,0:T(8,128)(2,1)S(1)} %collective-permute-done.2.refs_3_), channel_id=1, source_target_pairs={{4,0},{8,4},{12,8},{16,12},{20,16},{24,20},{28,24},{0,28},{5,1},{9... | collective-permute-start | bytes 614408 | tf_op jit(solution)/shard_map/ppermute | solution.py:26
  29.0 7.8 %collective-permute-start.6 = (bf16[400,256]{1,0:T(8,128)(2,1)S(1)}, bf16[400,256]{1,0:T(8,128)(2,1)S(1)}, u32[]{:S(2)}, u32[]{:S(2)}) collective-permute-start(bf16[400,256]{1,0:T(8,128)(2,1)S(1)} %collective-permute-done.4.refs_4_), channel_id=1, source_target_pairs={{28,0},{0,4},{4,8},{8,12},{12,16},{16,20},{20,24},{24,28},{29,1},{... | collective-permute-start | bytes 614408 | tf_op jit(solution)/shard_map/ppermute | solution.py:26
  36.0 14.9 %collective-permute-start.10 = (bf16[400,512]{1,0:T(8,128)(2,1)S(1)}, bf16[400,512]{1,0:T(8,128)(2,1)S(1)}, u32[]{:S(2)}, u32[]{:S(2)}) collective-permute-start(bf16[400,512]{1,0:T(8,128)(2,1)S(1)} %constant_dynamic-update-slice_fusion.2.refs_0_), channel_id=1, source_target_pairs={{32,0},{64,32},{96,64},{0,96},{33,1},{65,33},{97,65},{1,97},{34,2}... | collective-permute-start | bytes 1228808 | tf_op jit(solution)/shard_map/ppermute | solution.py:26
  36.8 7.0 %collective-permute-start.7 = (bf16[400,256]{1,0:T(8,128)(2,1)S(1)}, bf16[400,256]{1,0:T(8,128)(2,1)S(1)}, u32[]{:S(2)}, u32[]{:S(2)}) collective-permute-start(bf16[400,256]{1,0:T(8,128)(2,1)S(1)} %collective-permute-done.5.refs_5_), channel_id=1, source_target_pairs={{4,0},{8,4},{12,8},{16,12},{20,16},{24,20},{28,24},{0,28},{5,1},{9... | collective-permute-start | bytes 614408 | tf_op jit(solution)/shard_map/ppermute | solution.py:26
  58.3 22.5 %collective-permute-start.12 = (bf16[2,136,768]{2,1,0:T(8,128)(2,1)S(1)}, bf16[2,136,768]{2,1,0:T(8,128)(2,1)S(1)}, u32[]{:S(2)}, u32[]{:S(2)}) collective-permute-start(bf16[2,136,768]{2,1,0:T(8,128)(2,1)S(1)} %get-tuple-element.53), channel_id=1, source_target_pairs={{96,0},{0,32},{32,64},{64,96},{97,1},{1,33},{33,65},{65,97},{98,2}... | collective-permute-start | bytes 1253384 | tf_op jit(solution)/shard_map/ppermute | solution.py:26
  67.2 17.1 %collective-permute-start.14 = (bf16[2,136,768]{2,1,0:T(8,128)(2,1)S(1)}, bf16[2,136,768]{2,1,0:T(8,128)(2,1)S(1)}, u32[]{:S(2)}, u32[]{:S(2)}) collective-permute-start(bf16[2,136,768]{2,1,0:T(8,128)(2,1)S(1)} %get-tuple-element.55), channel_id=1, source_target_pairs={{32,0},{64,32},{96,64},{0,96},{33,1},{65,33},{97,65},{1,97},{34,2}... | collective-permute-start | bytes 1253384 | tf_op jit(solution)/shard_map/ppermute | solution.py:26
  67.2 17.1 %collective-permute-start.13 = (bf16[2,136,768]{2,1,0:T(8,128)(2,1)S(1)}, bf16[2,136,768]{2,1,0:T(8,128)(2,1)S(1)}, u32[]{:S(2)}, u32[]{:S(2)}) collective-permute-start(bf16[2,136,768]{2,1,0:T(8,128)(2,1)S(1)} %attend.3), channel_id=1, source_target_pairs={{64,0},{96,32},{0,64},{32,96},{65,1},{97,33},{1,65},{33,97},{66,2}... | collective-permute-start | bytes 1253384 | tf_op jit(solution)/shard_map/ppermute | solution.py:26
  84.9 7.4 %collective-permute-start.15 = (bf16[104,512]{1,0:T(8,128)(2,1)S(1)}, bf16[104,512]{1,0:T(8,128)(2,1)S(1)}, u32[]{:S(2)}, u32[]{:S(2)}) collective-permute-start(bf16[104,512]{1,0:T(8,128)(2,1)S(1)} %get-tuple-element.57), channel_id=1, source_target_pairs={{128,0},{0,128},{129,1},{1,129},{130,2},{2,130},{131,3},{3,131},{1... | collective-permute-start | bytes 319496 | tf_op jit(solution)/shard_map/ppermute | solution.py:26
  88.2 4.2 %collective-permute-start.16 = (bf16[104,512]{1,0:T(8,128)(2,1)S(1)}, bf16[104,512]{1,0:T(8,128)(2,1)S(1)}, u32[]{:S(2)}, u32[]{:S(2)}) collective-permute-start(bf16[104,512]{1,0:T(8,128)(2,1)S(1)} %get-tuple-element.58), channel_id=1, source_target_pairs={{1,0},{0,1},{3,2},{2,3},{5,4},{4,5},{7,6},{6,7},{9,8},{8,9},{11,10... | collective-permute-start | bytes 319496 | tf_op jit(solution)/shard_map/ppermute | solution.py:26
  88.2 6.1 %slice-start = ((s8[8388608]{0:T(1024)(128)(4,1)}), s8[4194304]{0:T(1024)(128)(4,1)S(1)}, s32[]{:S(2)}) async-start(s8[8388608]{0:T(1024)(128)(4,1)} %bitcast.10), calls=%async_computation | async-start | bytes 8388608
  88.2 6.1 %slice-start.1 = ((s8[8388608]{0:T(1024)(128)(4,1)}), s8[4194304]{0:T(1024)(128)(4,1)S(1)}, s32[]{:S(2)}) async-start(s8[8388608]{0:T(1024)(128)(4,1)} %bitcast.10), calls=%async_computation.1 | async-start | bytes 8388608
  88.2 6.1 %collective-permute-start.17 = (bf16[104,512]{1,0:T(8,128)(2,1)S(1)}, bf16[104,512]{1,0:T(8,128)(2,1)S(1)}, u32[]{:S(2)}, u32[]{:S(2)}) collective-permute-start(bf16[104,512]{1,0:T(8,128)(2,1)S(1)} %get-tuple-element.59), channel_id=1, source_target_pairs={{0,129},{1,128},{128,1},{129,0},{2,131},{3,130},{130,3},{131,2},{4... | collective-permute-start | bytes 319496 | tf_op jit(solution)/shard_map/ppermute | solution.py:539
  97.3 11.9 %collective-permute-start.20 = (bf16[48,2176]{1,0:T(8,128)(2,1)S(1)}, bf16[48,2176]{1,0:T(8,128)(2,1)S(1)}, u32[]{:S(2)}, u32[]{:S(2)}) collective-permute-start(bf16[48,2176]{1,0:T(8,128)(2,1)S(1)} %get-tuple-element.69), channel_id=1, source_target_pairs={{2,0},{0,2},{3,1},{1,3},{6,4},{4,6},{7,5},{5,7},{10,8},{8,10},{11,... | collective-permute-start | bytes 626696 | tf_op jit(solution)/shard_map/ppermute | solution.py:26
  98.0 11.1 %collective-permute-start.19 = (bf16[48,2048]{1,0:T(8,128)(2,1)S(1)}, bf16[48,2048]{1,0:T(8,128)(2,1)S(1)}, u32[]{:S(2)}, u32[]{:S(2)}) collective-permute-start(bf16[48,2048]{1,0:T(8,128)(2,1)S(1)} %get-tuple-element.68), channel_id=1, source_target_pairs={{2,0},{0,2},{3,1},{1,3},{6,4},{4,6},{7,5},{5,7},{10,8},{8,10},{11,... | collective-permute-start | bytes 589832 | tf_op jit(solution)/shard_map/ppermute | solution.py:26
